TPU v7x, 32 devices: a whole 2x2x4 slice. The times are simulated.
32 devices in a mesh: dp: 4 (over y, x), expert: 8 (over z, core).
Axes of the slice: x: 2, y: 2, z: 4, core: 2. Of those that a mesh axis runs over, the one named last changes fastest.
Arguments:
- tokens: bfloat16 [4096, 4096], P(('dp', 'expert')), may hold values from -6 to 6
- routes: int32 [4096, 2], P(('dp', 'expert')), may hold values from 0 to 7, all different within a row; in each aligned block of 128 rows (0 to 127, 128 to 255, ...) at most 48 rows name the same one
- router_weight: bfloat16 [4096, 8], replicated, may hold values from -0.09375 to 0.09375
- shift: float32 [1, 4096], replicated, may hold values from -3 to 3
- scale: float32 [1, 4096], replicated, may hold values from -3 to 3
- gate_mod: float32 [1, 4096], replicated, may hold values from -4 to 4
- gate_weight: bfloat16 [8, 4096, 1024], P(None, ('dp', 'expert')), may hold values from -0.09375 to 0.09375
- up_weight: bfloat16 [8, 4096, 1024], P(None, ('dp', 'expert')), may hold values from -0.09375 to 0.09375
- down_weight: bfloat16 [8, 4096, 1024], P(None, ('dp', 'expert')), may hold values from -0.1875 to 0.1875
Outputs:
- update: bfloat16 [4096, 4096], P(('dp', 'expert'))
Inputs may be any that keep to these rules, and one draw needn't show every extreme that they name: `routes`: each row names two different experts; among the rows of one device no expert is named more than 48 times, a bound that some block reaches.
All inputs are finite; a program needn't handle non-finite values.
Results may differ from a plain program's by a relative error of at most 0.0072.
Values may be sent and summed in bfloat16 or wider, within the bound.
No kernel may reach another device: no remote copies, remote signals or barrier semaphores. Data moves between devices by JAX's collectives and lax.ppermute only.
A program may use at most 128 MiB of HBM per device.

v0:
```python
import jax
import jax.numpy as jnp
from jax import lax
from jax.experimental import pallas as pl
from jax.experimental.pallas import tpu as pltpu
from jax.sharding import PartitionSpec as P


PIX = 4096
EPS = 1e-06
AXES = ("dp", "expert")
CORES = 2
LANES = 128
PIECES = 1


def send_back(output):
    return lax.all_to_all(output, "expert", split_axis=0, concat_axis=0, tiled=True)


def routed_shards(
    tokens, routes, router_weight, shift, scale, gate_mod, gate_weight, up_weight, down_weight
):
    tok_dev = tokens.shape[0]
    width = tokens.shape[1]
    experts = router_weight.shape[1]
    n_owner = lax.axis_size("expert")
    local_count = experts // n_owner
    capacity = max(2, 3 * tok_dev // experts)
    first_row = (lax.axis_index("dp") * n_owner + lax.axis_index("expert")) * tok_dev
    image = first_row // PIX
    shift_row = lax.dynamic_slice_in_dim(shift, image, 1, 0)
    scale_row = lax.dynamic_slice_in_dim(scale, image, 1, 0)
    gate_row = lax.dynamic_slice_in_dim(gate_mod, image, 1, 0)
    values = tokens.astype(jnp.float32)
    meansq = jnp.mean(values * values, axis=-1, keepdims=True)
    normed = (values * lax.rsqrt(meansq + EPS) * (1.0 + scale_row) + shift_row).astype(jnp.bfloat16)
    logits = jnp.dot(normed, router_weight, preferred_element_type=jnp.float32)
    onehot = routes[:, :, None] == jnp.arange(experts, dtype=jnp.int32)[None, None, :]
    chosen = jnp.sum(jnp.where(onehot, logits[:, None, :], 0.0), axis=-1)
    score = jax.nn.sigmoid(chosen)
    flat = routes.reshape(-1)
    hot = (flat[:, None] == jnp.arange(experts, dtype=jnp.int32)[None, :]).astype(jnp.int32)
    rank = jnp.cumsum(hot, axis=0) - hot
    slot = jnp.sum(rank * hot, axis=-1)
    position = flat * capacity + slot
    source = (
        jnp.zeros((experts * capacity,), jnp.int32)
        .at[position]
        .set(jnp.arange(2 * tok_dev, dtype=jnp.int32) // 2)
    )
    filled = jnp.zeros((experts * capacity,), jnp.bool_).at[position].set(True)
    outgoing = jnp.where(filled[:, None], normed[source], jnp.zeros((), jnp.bfloat16)).reshape(
        experts, capacity, width
    )
    quarter_gate, quarter_up, quarter_down = (
        lax.all_to_all(gate_weight, "expert", split_axis=0, concat_axis=1, tiled=True),
        lax.all_to_all(up_weight, "expert", split_axis=0, concat_axis=1, tiled=True),
        lax.all_to_all(down_weight, "expert", split_axis=0, concat_axis=1, tiled=True),
    )
    w_gate, w_up, w_down = (
        lax.all_gather(quarter_gate, "dp", axis=1, tiled=True),
        lax.all_gather(quarter_up, "dp", axis=1, tiled=True),
        lax.all_gather(quarter_down, "dp", axis=1, tiled=True),
    )
    received = lax.all_to_all(outgoing, "expert", split_axis=0, concat_axis=0, tiled=True)
    slots = received.shape[1]
    grid = received.reshape(n_owner, local_count, slots, width)
    gate = jnp.einsum("nxcd,xdf->nxcf", grid, w_gate, preferred_element_type=jnp.float32)
    upper = jnp.einsum("nxcd,xdf->nxcf", grid, w_up, preferred_element_type=jnp.float32)
    hidden = (jax.nn.silu(gate) * upper).astype(jnp.bfloat16)
    output = jnp.einsum(
        "nxcf,xdf->nxcd", hidden, w_down, preferred_element_type=jnp.float32
    ).astype(jnp.bfloat16)
    output = output.reshape(n_owner * local_count, slots, width)
    incoming = send_back(output)
    picked = (
        incoming.reshape(experts * capacity, width)[position]
        .astype(jnp.float32)
        .reshape(tok_dev, 2, width)
    )
    branch = jnp.sum(score[:, :, None] * picked, axis=1)
    return (gate_row * branch).astype(jnp.bfloat16)


def prep_kernel(here, tok_ref, routes_ref, router_ref, shift_ref, scale_ref, *refs):
    outs, norm_ref = refs[:-1], refs[-1]
    z, c = here[1], here[2]
    planes = len(outs)
    tokens, width = tok_ref.shape
    quarter = width // planes
    experts = router_ref.shape[0]
    values = tok_ref[...].astype(jnp.float32)
    meansq = jnp.mean(values * values, axis=-1, keepdims=True)
    normed = values * lax.rsqrt(meansq + EPS) * (1.0 + scale_ref[...]) + shift_ref[...]
    normed = normed.astype(jnp.bfloat16)
    norm_ref[...] = normed
    logits = lax.dot_general(
        normed, router_ref[...], (((1,), (1,)), ((), ())), preferred_element_type=jnp.float32
    )
    ids = lax.broadcasted_iota(jnp.int32, (tokens, experts), 1)
    lane = lax.broadcasted_iota(jnp.int32, (tokens, LANES), 1)
    info = jnp.zeros((tokens, LANES), jnp.float32)
    for k in range(2):
        expert = routes_ref[:, k : k + 1]
        chosen = jnp.sum(jnp.where(ids == expert, logits, 0.0), axis=-1, keepdims=True)
        score = jax.nn.sigmoid(chosen)
        coarse = score.astype(jnp.bfloat16).astype(jnp.float32)
        info = jnp.where(lane == k, expert.astype(jnp.float32), info)
        info = jnp.where(lane == 2 + 2 * k, coarse, info)
        info = jnp.where(lane == 3 + 2 * k, score - coarse, info)
    info = info.astype(jnp.bfloat16)
    rows = LANES
    groups = quarter // (CORES * rows)
    for m, out in enumerate(outs):
        for side in range(CORES):
            for b in range(groups):
                start = ((b * planes + (z ^ m)) * CORES + (c ^ side)) * rows
                at = (side * groups + b) * rows
                out[:, at : at + rows] = norm_ref[:, pl.ds(pl.multiple_of(start, LANES), rows)]
        out[:, quarter:] = info


def prep(here, tokens, routes, router, shift_row, scale_row, planes):
    rows, width = tokens.shape
    block = jax.ShapeDtypeStruct((rows, width // planes + LANES), jnp.bfloat16)
    vmem = pl.BlockSpec(memory_space=pltpu.VMEM)
    return pl.pallas_call(
        prep_kernel,
        in_specs=[pl.BlockSpec(memory_space=pltpu.SMEM)] + [vmem] * 5,
        out_specs=[vmem] * planes,
        out_shape=[block] * planes,
        scratch_shapes=[pltpu.VMEM((rows, width), jnp.bfloat16)],
        name="prep",
    )(here, tokens, routes, router, shift_row, scale_row)


def product_kernel(groups, here, *refs):
    blocks, (first, second), outs, x_ref = refs[:groups], refs[groups : groups + 2], refs[groups + 2 : -1], refs[-1]
    experts, hid = first.shape[1], first.shape[-1]
    each = groups // len(outs)
    tile = blocks[0].shape[0]
    depth = x_ref.shape[1]
    half = depth // CORES
    for i, block in enumerate(blocks):
        at = slice(i * tile, (i + 1) * tile)
        for side in range(CORES):
            for m in range(groups):
                start = pl.multiple_of((side * groups + (here[0] ^ m)) * LANES, LANES)
                to = (side * groups + m) * LANES
                x_ref[at, to : to + LANES] = block[:, pl.ds(start, LANES)]
    routes = [[block[:, depth + k : depth + k + 1].astype(jnp.float32) for k in range(2)] for block in blocks]

    def expert(e, carry):
        mine = e.astype(jnp.float32)
        for part in range(2):
            to = slice(part * hid // 2, (part + 1) * hid // 2)
            weight = jnp.concatenate(
                [ref[:, e, :, to].reshape(half, hid // 2) for ref in (first, second)], axis=0
            )
            product = jnp.dot(x_ref[...], weight, preferred_element_type=jnp.float32)
            for i in range(groups):
                at, out_ref = slice(i % each * tile, (i % each + 1) * tile), outs[i // each]
                for k in range(2):
                    to = slice((2 * k + part) * hid // 2, (2 * k + part + 1) * hid // 2)
                    kept = out_ref[at, to].astype(jnp.float32)
                    value = product[i * tile : (i + 1) * tile]
                    out_ref[at, to] = jnp.where(routes[i][k] == mine, value, kept).astype(jnp.bfloat16)
        return carry

    lax.fori_loop(0, experts, expert, 0, unroll=2)


def expert_product(here, blocks, weights):
    groups, experts, _, hid = weights[0].shape
    tile, lanes = blocks[0].shape
    tokens = groups * tile
    depth = lanes - LANES
    vmem = pl.BlockSpec(memory_space=pltpu.VMEM)
    return pl.pallas_call(
        lambda *refs: product_kernel(groups, *refs),
        in_specs=[pl.BlockSpec(memory_space=pltpu.SMEM)] + [vmem] * (groups + 2),
        out_specs=[vmem] * PIECES,
        out_shape=[jax.ShapeDtypeStruct((tokens // PIECES, 2 * hid), jnp.bfloat16)] * PIECES,
        scratch_shapes=[pltpu.VMEM((tokens, depth), jnp.bfloat16)],
        cost_estimate=pl.CostEstimate(
            flops=experts * 2 * tokens * depth * hid, transcendentals=0, bytes_accessed=4 * weights[0].size
        ),
        compiler_params=pltpu.CompilerParams(vmem_limit_bytes=24 * 2**20),
        name="product",
    )(here, *blocks, *weights)


def hidden_kernel(groups, count, *refs):
    pieces, blocks, out_ref = refs[: count * PIECES], refs[count * PIECES : -1], refs[-1]
    each = groups // PIECES
    hid = out_ref.shape[1] // 2
    tile, lanes = blocks[0].shape
    depth = lanes - LANES
    for i, block in enumerate(blocks):
        at = slice(i % each * tile, (i % each + 1) * tile)
        parts = pieces[i // each :: PIECES]
        for k in range(2):
            score = [block[:, depth + 2 + 2 * k + n : depth + 3 + 2 * k + n].astype(jnp.float32) for n in range(2)]
            sums = []
            for part in range(2):
                to = slice((2 * k + part) * hid, (2 * k + part + 1) * hid)
                total = parts[0][at, to].astype(jnp.float32)
                for other in parts[1:]:
                    total = total + other[at, to].astype(jnp.float32)
                sums.append(total)
            value = sums[0] / (1.0 + jnp.exp(-sums[0])) * sums[1] * (score[0] + score[1])
            out_ref[i * tile : (i + 1) * tile, k * hid : (k + 1) * hid] = value.astype(jnp.bfloat16)


def hidden_rows(parts, blocks):
    groups = len(blocks)
    tokens, columns = parts[0][0].shape[0] * PIECES, parts[0][0].shape[1]
    flat = [piece for part in parts for piece in part]
    vmem = pl.BlockSpec(memory_space=pltpu.VMEM)
    return pl.pallas_call(
        lambda *refs: hidden_kernel(groups, len(parts), *refs),
        in_specs=[vmem] * (len(flat) + groups),
        out_specs=vmem,
        out_shape=jax.ShapeDtypeStruct((tokens, columns // 2), jnp.bfloat16),
        cost_estimate=pl.CostEstimate(flops=10**9, transcendentals=0, bytes_accessed=4 * tokens * columns),
        name="hidden",
    )(*flat, *blocks)


def down_kernel(groups, experts, halves, here, *refs):
    hiddens, blocks, refs = refs[:halves], refs[halves : halves + groups], refs[halves + groups :]
    down_a, down_b, outs, wide_ref = refs[0], refs[1], refs[2 : 2 + groups], refs[-1]
    part = hiddens[0].shape[1] // 2
    hid = part * halves
    tile, lanes = blocks[0].shape
    depth = lanes - LANES
    pair = 2 if groups % 2 == 0 else 1
    zero = jnp.zeros((), jnp.float32)
    for i, block in enumerate(blocks):
        at = slice(i * tile, (i + 1) * tile)
        routes = [block[:, depth + k : depth + k + 1].astype(jnp.float32) for k in range(2)]
        for h, ref in enumerate(hiddens):
            rows = [ref[at, k * part : (k + 1) * part].astype(jnp.float32) for k in range(2)]
            for e in range(experts):
                value = jnp.where(routes[0] == float(e), rows[0], zero)
                value = jnp.where(routes[1] == float(e), rows[1], value)
                to = e * hid + h * part
                wide_ref[at, to : to + part] = value.astype(jnp.bfloat16)
    for side, ref in enumerate((down_a, down_b)):
        for j in range(0, groups, pair):
            weight = jnp.concatenate(
                [jnp.concatenate([ref[j + p, e] for p in range(pair)], axis=0) for e in range(experts)], axis=1
            )
            product = lax.dot_general(
                wide_ref[...], weight, (((1,), (1,)), ((), ())), preferred_element_type=jnp.float32
            ).astype(jnp.bfloat16)
            for p in range(pair):
                start = pl.multiple_of((side * groups + (here[0] ^ (j + p))) * LANES, LANES)
                for i, out in enumerate(outs):
                    out[:, pl.ds(start, LANES)] = product[i * tile : (i + 1) * tile, p * LANES : (p + 1) * LANES]


def down_product(here, hiddens, blocks, down):
    groups, experts, _, hid = down[0].shape
    tile, lanes = blocks[0].shape
    tokens = groups * tile
    width = lanes - LANES
    vmem = pl.BlockSpec(memory_space=pltpu.VMEM)
    return pl.pallas_call(
        lambda *refs: down_kernel(groups, experts, len(hiddens), *refs),
        in_specs=[pl.BlockSpec(memory_space=pltpu.SMEM)] + [vmem] * (len(hiddens) + groups + 2),
        out_specs=[vmem] * groups,
        out_shape=[jax.ShapeDtypeStruct((tile, width), jnp.bfloat16)] * groups,
        scratch_shapes=[pltpu.VMEM((tokens, experts * hid), jnp.bfloat16)],
        cost_estimate=pl.CostEstimate(
            flops=experts * 2 * tokens * width * hid, transcendentals=0, bytes_accessed=2 * down[0].size * 2
        ),
        compiler_params=pltpu.CompilerParams(vmem_limit_bytes=24 * 2**20),
        name="down",
    )(here, *hiddens, *blocks, *down)


def combine_kernel(groups, planes, here, gate_ref, *refs):
    parts, out_ref = refs[:-1], refs[-1]
    z, c = here[1], here[2]
    for side in range(CORES):
        for b in range(groups):
            to = slice((side * groups + b) * LANES, (side * groups + b + 1) * LANES)
            total = parts[0][:, to].astype(jnp.float32)
            for part in parts[1:]:
                total = total + part[:, to].astype(jnp.float32)
            start = pl.multiple_of(((b * planes + z) * CORES + (c ^ side)) * LANES, LANES)
            out_ref[:, to] = (total * gate_ref[:, pl.ds(start, LANES)]).astype(jnp.bfloat16)


def combine(here, gate_row, parts, planes):
    vmem = pl.BlockSpec(memory_space=pltpu.VMEM)
    return pl.pallas_call(
        lambda *refs: combine_kernel(len(parts), planes, *refs),
        in_specs=[pl.BlockSpec(memory_space=pltpu.SMEM)] + [vmem] * (1 + len(parts)),
        out_specs=vmem,
        out_shape=jax.ShapeDtypeStruct(parts[0].shape, jnp.bfloat16),
        name="combine",
    )(here, gate_row, *parts)


def place_kernel(groups, here, *refs):
    pieces, out_ref = refs[:-1], refs[-1]
    planes = len(pieces)
    z, c = here[1], here[2]
    for m, piece in enumerate(pieces):
        for side in range(CORES):
            for b in range(groups):
                start = pl.multiple_of(((b * planes + (z ^ m)) * CORES + (c ^ side)) * LANES, LANES)
                at = (side * groups + b) * LANES
                out_ref[:, pl.ds(start, LANES)] = piece[:, at : at + LANES]


def place(here, pieces, groups):
    tokens, quarter = pieces[0].shape
    vmem = pl.BlockSpec(memory_space=pltpu.VMEM)
    return pl.pallas_call(
        lambda *refs: place_kernel(groups, *refs),
        in_specs=[pl.BlockSpec(memory_space=pltpu.SMEM)] + [vmem] * len(pieces),
        out_specs=vmem,
        out_shape=jax.ShapeDtypeStruct((tokens, quarter * len(pieces)), jnp.bfloat16),
        name="place",
    )(here, *pieces)


def plane_shards(groups, owners):
    planes = owners // CORES

    def flat(g, z, c):
        return (g * planes + z) * CORES + c

    def permute(value, move):
        pairs = []
        for g in range(groups):
            for z in range(planes):
                for c in range(CORES):
                    to = move(g, z, c)
                    if to is not None:
                        pairs.append((flat(g, z, c), flat(*to)))
        return lax.ppermute(value, AXES, pairs)

    def across(value, m):
        return permute(value, lambda g, z, c: (g ^ m, z, c))

    def along(value, m):
        return permute(value, lambda g, z, c: (g, z ^ m, c))

    def swap(value):
        return permute(value, lambda g, z, c: (g, z, c ^ 1))

    def upward(value, senders):
        return permute(value, lambda g, z, c: (g, z + 1, c) if z in senders else None)

    def downward(value, senders):
        return permute(value, lambda g, z, c: (g, z - 1, c) if z in senders else None)

    def after(value, other):
        return lax.optimization_barrier((value, other))[0]

    def add(first, second):
        return (first.astype(jnp.float32) + second.astype(jnp.float32)).astype(jnp.bfloat16)

    def shards_of(tokens, routes, router_weight, shift, scale, gate_mod, gate_weight, up_weight, down_weight):
        tok_dev = tokens.shape[0]
        hid = gate_weight.shape[2] // groups
        g = lax.axis_index("dp")
        owner = lax.axis_index("expert")
        z, c = owner // CORES, owner % CORES
        here = jnp.stack([g, z, c]).astype(jnp.int32)

        def among(names):
            found = jnp.zeros((), jnp.bool_)
            for plane in names:
                found = found | (z == plane)
            return found

        def pick(slots, choice):
            names = sorted(set(choice.values()))
            value = slots[names[0]]
            for name in names[1:]:
                value = jnp.where(among([p for p, slot in choice.items() if slot == name]), slots[name], value)
            return value

        def row_of(table, m):
            image = flat(g, z ^ m, c) * tok_dev // PIX
            return lax.dynamic_slice_in_dim(table, image, 1, 0)

        def share(*weights, columns, start):
            def part(m):
                pieces = [lax.dynamic_slice_in_dim(w, (g ^ m) * hid + start, columns, 2) for w in weights]
                return jnp.concatenate(pieces, axis=2) if len(pieces) > 1 else pieces[0]

            return [part(m) for m in range(groups)]

        def send(parts):
            return parts[:1] + [across(parts[m], m) for m in range(1, groups)]

        far = planes - 1
        order = list(range(far, -1, -1))

        parts0 = send(share(gate_weight, up_weight, columns=hid, start=0))
        split = prep(here, tokens, routes, router_weight.T, row_of(shift, 0), row_of(scale, 0), planes)
        sent = {0: split[0]}
        for m in order[:-1]:
            sent[m] = along(split[m], m)
        cut2 = share(after(down_weight, split), columns=hid, start=0)
        blocks = {}
        for m in order:
            blocks[m] = [sent[m]] + [across(sent[m], b) for b in range(1, groups)]
        parts2 = send(cut2)

        def stack(parts, done):
            full = jnp.stack(after(parts, done))
            return full, (full, swap(full))

        def multiply(m, weights, done):
            return expert_product(here, after(blocks[m], done), weights)

        def moved(s, partial, arrived, done):
            climb = {p: p ^ (planes - s + p) for p in range(0, s)}
            sink = {p: p ^ (s - planes + p) for p in range(planes - s, planes)}
            news = []
            for r in range(PIECES):
                mine = {m: pieces[r] for m, pieces in partial.items()}
                below, above = after(arrived[r], done) if arrived is not None else (None, None)
                if set(climb) & set(sink):
                    rising, falling = pick(mine, climb), pick(mine, sink)
                    if below is not None:
                        rising, falling = add(rising, below), add(falling, above)
                else:
                    rising = pick(mine, {**climb, **sink})
                    if below is not None:
                        rising = add(rising, jnp.where(among(climb), below, above))
                    falling = rising
                done = (rising, falling)
                news.append((upward(rising, set(climb)), downward(falling, set(sink))))
            return news, done

        last, weights = stack(parts0, cut2)
        partial = {far: multiply(far, weights, last)}
        sums, _ = moved(1, {m: partial[far] for m in order}, None, None)
        last = partial[far]
        for m in order[1:-1]:
            last = partial[m] = multiply(m, weights, last)
        whole = {m: partial.get(m, last) for m in order}
        for s in range(2, far):
            sums, last = moved(s, whole, sums, last)
        last = partial[0] = multiply(0, weights, last)
        last, down_full = stack(parts2, last)
        if far > 1:
            sums, last = moved(far, partial, sums, last)
        arrived = after(sums, last)
        belows, aboves = [one[0] for one in arrived], [one[1] for one in arrived]
        hidden = hidden_rows([partial[0], belows, aboves], blocks[0])
        last = hidden
        rows_in = {0: hidden}
        for m in order[:-1]:
            rows_in[m] = along(hidden, m)

        parts, finished = {}, {}

        def finish(m, done):
            piece = combine(here, row_of(gate_mod, m), after(parts[m], done), planes)
            finished[m] = along(piece, m) if m else piece
            return piece

        waiting = []
        for m in range(planes):
            last = out = down_product(here, after([rows_in[m]], last), blocks[m], down_full)
            parts[m] = [out[0]] + [across(out[b], b) for b in range(1, groups)]
            if waiting:
                last = finish(waiting.pop(0), last)
            waiting.append(m)
        for m in waiting:
            last = finish(m, last)
        return place(here, [finished[m] for m in range(planes)], groups)

    return shards_of


def solution(mesh):
    groups, owners = mesh.shape["dp"], mesh.shape["expert"]

    def program(tokens, routes, router_weight, shift, scale, gate_mod, gate_weight, up_weight, down_weight):
        rows = P(AXES, None)
        weights = P(None, AXES, None)
        in_specs = (rows, rows, P(), P(), P(), P(), weights, weights, weights)
        planes = owners // CORES
        whole_lanes = gate_weight.shape[1] == LANES * groups * owners
        powers = groups & (groups - 1) == 0 and planes & (planes - 1) == 0 and owners == planes * CORES
        whole = whole_lanes and powers and planes > 2 and groups > 1 and gate_weight.shape[2] % (2 * LANES * groups) == 0
        body = plane_shards(groups, owners) if whole else routed_shards
        step = jax.shard_map(body, mesh=mesh, in_specs=in_specs, out_specs=rows, check_vma=False)
        return step(tokens, routes, router_weight, shift, scale, gate_mod, gate_weight, up_weight, down_weight)

    return program
```

profile of v0, /device:TPU:0, one launch (start us, length us, event | category | flops | bytes accessed | tf_op | source)
XLA Modules:
  0.0 292.2 jit_solution(1649794796894655349)
XLA Ops:
  0.0 2.6 constant_dynamic-slice_fusion.4
  3.7 3.0 %collective-permute-start.11 = (bf16[8,128,512]{2,1,0:T(8,128)(2,1)}, bf16[8,128,512]{2,1,0:T(8,128)(2,1)}, u32[]{:S(2)}, u32[]{:S(2)}) collective-permute-start(bf16[8,128,512]{2,1,0:T(8,128)(2,1)} %pad_maximum_fusion.3), channel_id=1, source_target_pairs={{0,8},{1,9},{2,10},{3,11},{4,12},{5,13},{6,14},{7,15},{8,0},{9,1},... | collective-permute-start | bytes 3145736 | tf_op jit(solution)/shard_map/ppermute | solution.py:346
  11.7 3.3 %prep.1 = (bf16[128,1152]{1,0:T(8,128)(2,1)}, bf16[128,1152]{1,0:T(8,128)(2,1)}, bf16[128,1152]{1,0:T(8,128)(2,1)}, bf16[128,1152]{1,0:T(8,128)(2,1)}) custom-call(s32[3]{0:T(128)} %pad_add_fusion.here.refs_0_, bf16[128,4096]{1,0:T(8,128)(2,1)} %tok_ref.1, s32[128,2]{1,0:T(8,128)} %copy.10.routes_ref, bf16[8,4096]{1,0:T(8,128)(2,1)} %bitcast.17, ...), custom_call_target="tpu_custom_call" | custom-call | tf_op jit(solution)/shard_map/prep/pallas_call | solution.py:128
  16.6 14.4 %collective-permute-done.11 = bf16[8,128,512]{2,1,0:T(8,128)(2,1)} collective-permute-done((bf16[8,128,512]{2,1,0:T(8,128)(2,1)}, bf16[8,128,512]{2,1,0:T(8,128)(2,1)}, u32[]{:S(2)}, u32[]{:S(2)}) %collective-permute-start.11) | collective-permute-done | bytes 1048608 | tf_op jit(solution)/shard_map/ppermute | solution.py:346
  31.0 24.2 %collective-permute-done.12 = bf16[8,128,512]{2,1,0:T(8,128)(2,1)} collective-permute-done((bf16[8,128,512]{2,1,0:T(8,128)(2,1)}, bf16[8,128,512]{2,1,0:T(8,128)(2,1)}, u32[]{:S(2)}, u32[]{:S(2)}) %collective-permute-start.12) | collective-permute-done | bytes 1048608 | tf_op jit(solution)/shard_map/ppermute | solution.py:346
  55.2 2.2 pad_maximum_fusion.refs_5_
  57.5 3.7 %collective-permute-start.7 = (bf16[128,1152]{1,0:T(8,128)(2,1)S(1)}, bf16[128,1152]{1,0:T(8,128)(2,1)S(1)}, u32[]{:S(2)}, u32[]{:S(2)}) collective-permute-start(bf16[128,1152]{1,0:T(8,128)(2,1)S(1)} %copy-done.63), channel_id=1, source_target_pairs={{0,6},{1,7},{2,4},{3,5},{4,2},{5,3},{6,0},{7,1},{8,14},{9,15},{10,... | collective-permute-start | bytes 884744 | tf_op jit(solution)/shard_map/ppermute | solution.py:346
  61.2 8.2 %collective-permute-done.7.refs_1_.refs_2_ = bf16[128,1152]{1,0:T(8,128)(2,1)S(1)} collective-permute-done((bf16[128,1152]{1,0:T(8,128)(2,1)S(1)}, bf16[128,1152]{1,0:T(8,128)(2,1)S(1)}, u32[]{:S(2)}, u32[]{:S(2)}) %collective-permute-start.7) | collective-permute-done | bytes 294944 | tf_op jit(solution)/shard_map/ppermute | solution.py:346
  72.8 14.0 %collective-permute-done.3.refs_1_.refs_2_ = bf16[128,1152]{1,0:T(8,128)(2,1)S(1)} collective-permute-done((bf16[128,1152]{1,0:T(8,128)(2,1)S(1)}, bf16[128,1152]{1,0:T(8,128)(2,1)S(1)}, u32[]{:S(2)}, u32[]{:S(2)}) %collective-permute-start.3) | collective-permute-done | bytes 294944 | tf_op jit(solution)/shard_map/ppermute | solution.py:346
  90.5 6.5 %product.4 = bf16[512,1024]{1,0:T(8,128)(2,1)S(1)} custom-call(s32[3]{0:T(128)S(1)} %copy-done.17, bf16[128,1152]{1,0:T(8,128)(2,1)S(1)} %collective-permute-done.7.refs_1_.refs_2_, bf16[128,1152]{1,0:T(8,128)(2,1)S(1)} %collective-permute-done.8.refs_2_.refs_3_, bf16[128,1152]{1,0:T(8,128)(2,1)S(1)} %collective-permute-done.9.refs_3_.refs_4_, ...), custom_call_target="tpu_custom_call" | custom-call | flops 4294967296 | bytes 8388608 | tf_op jit(solution)/shard_map/product/pallas_call | solution.py:180
  97.0 13.3 %collective-permute-start.15 = (bf16[512,1024]{1,0:T(8,128)(2,1)S(1)}, bf16[512,1024]{1,0:T(8,128)(2,1)}, u32[]{:S(2)}, u32[]{:S(2)}) collective-permute-start(bf16[512,1024]{1,0:T(8,128)(2,1)S(1)} %product.4), channel_id=1, source_target_pairs={{0,2},{1,3},{8,10},{9,11},{16,18},{17,19},{24,26},{25,27}} | collective-permute-start | bytes 3145736 | tf_op jit(solution)/shard_map/ppermute | solution.py:346
  110.3 1.6 collective-permute-start.16
  115.5 2.2 copy-done.1
  117.6 2.2 copy-done.21
  119.8 6.4 %product.5 = bf16[512,1024]{1,0:T(8,128)(2,1)S(1)} custom-call(s32[3]{0:T(128)S(1)} %copy-done.17, bf16[128,1152]{1,0:T(8,128)(2,1)S(1)} %collective-permute-done.3.refs_1_.refs_2_, bf16[128,1152]{1,0:T(8,128)(2,1)S(1)} %collective-permute-done.4.refs_2_.refs_3_, bf16[128,1152]{1,0:T(8,128)(2,1)S(1)} %collective-permute-done.5.refs_3_.refs_4_, ...), custom_call_target="tpu_custom_call" | custom-call | flops 4294967296 | bytes 8388608 | tf_op jit(solution)/shard_map/product/pallas_call | solution.py:180
  126.3 1.6 collective-permute-start
  129.9 6.4 %product.6 = bf16[512,1024]{1,0:T(8,128)(2,1)S(1)} custom-call(s32[3]{0:T(128)S(1)} %copy-done.17, bf16[128,1152]{1,0:T(8,128)(2,1)S(1)} %collective-permute-done.17.refs_1_.refs_2_, bf16[128,1152]{1,0:T(8,128)(2,1)S(1)} %collective-permute-done.18.refs_2_.refs_3_, bf16[128,1152]{1,0:T(8,128)(2,1)S(1)} %collective-permute-done.19.refs_3_.refs_4_, ...), custom_call_target="tpu_custom_call" | custom-call | flops 4294967296 | bytes 8388608 | tf_op jit(solution)/shard_map/product/pallas_call | solution.py:180
  136.3 3.3 %add_convert_fusion.2 = bf16[512,1024]{1,0:T(8,128)(2,1)} fusion(bf16[512,1024]{1,0:T(8,128)(2,1)S(1)} %product.5, bf16[512,1024]{1,0:T(8,128)(2,1)} %collective-permute-done.15, bf16[512,1024]{1,0:T(8,128)(2,1)} %collective-permute-done.16, pred[]{:T(512)S(6)} %or.3), kind=kLoop, calls=%fused_computation.4 | loop fusion | flops 2621440 | bytes 4194305 | tf_op jit(solution)/shard_map/convert_element_type | solution.py:367
  139.6 2.4 collective-permute-start.21
  142.0 1.7 collective-permute-start.22
  143.7 1.5 collective-permute-start.23
  145.8 1.5 collective-permute-start.25
  147.4 6.4 %product.7.refs_0_ = bf16[512,1024]{1,0:T(8,128)(2,1)S(1)} custom-call(s32[3]{0:T(128)S(1)} %copy-done.17, bf16[128,1152]{1,0:T(8,128)(2,1)S(1)} %copy-done.5, bf16[128,1152]{1,0:T(8,128)(2,1)S(1)} %collective-permute-done.refs_2_.refs_4_.refs_3_, bf16[128,1152]{1,0:T(8,128)(2,1)S(1)} %collective-permute-done.1.refs_3_.refs_5_.refs_4_, ...), custom_call_target="tpu_custom_call" | custom-call | flops 4294967296 | bytes 8388608 | tf_op jit(solution)/shard_map/product/pallas_call | solution.py:180
  153.8 4.6 %collective-permute-done.23 = bf16[8,128,256]{2,1,0:T(8,128)(2,1)S(1)} collective-permute-done((bf16[8,128,256]{2,1,0:T(8,128)(2,1)S(1)}, bf16[8,128,256]{2,1,0:T(8,128)(2,1)S(1)}, u32[]{:S(2)}, u32[]{:S(2)}) %collective-permute-start.23) | collective-permute-done | bytes 524320 | tf_op jit(solution)/shard_map/ppermute | solution.py:346
  158.4 6.9 %collective-permute-done.24 = bf16[8,128,256]{2,1,0:T(8,128)(2,1)S(1)} collective-permute-done((bf16[8,128,256]{2,1,0:T(8,128)(2,1)S(1)}, bf16[8,128,256]{2,1,0:T(8,128)(2,1)S(1)}, u32[]{:S(2)}, u32[]{:S(2)}) %collective-permute-start.24) | collective-permute-done | bytes 524320 | tf_op jit(solution)/shard_map/ppermute | solution.py:346
  165.7 2.8 add_convert_fusion
  168.5 2.4 collective-permute-start.26
  172.4 20.7 %collective-permute-done.26.refs_1_ = bf16[512,1024]{1,0:T(8,128)(2,1)} collective-permute-done((bf16[512,1024]{1,0:T(8,128)(2,1)S(1)}, bf16[512,1024]{1,0:T(8,128)(2,1)}, u32[]{:S(2)}, u32[]{:S(2)}) %collective-permute-start.26) | collective-permute-done | bytes 1048608 | tf_op jit(solution)/shard_map/ppermute | solution.py:346
  193.2 5.3 %collective-permute-done.27.refs_2_ = bf16[512,1024]{1,0:T(8,128)(2,1)} collective-permute-done((bf16[512,1024]{1,0:T(8,128)(2,1)S(1)}, bf16[512,1024]{1,0:T(8,128)(2,1)}, u32[]{:S(2)}, u32[]{:S(2)}) %collective-permute-start.27) | collective-permute-done | bytes 1048608 | tf_op jit(solution)/shard_map/ppermute | solution.py:346
  198.5 3.8 %hidden.1.refs_1_ = bf16[512,512]{1,0:T(8,128)(2,1)} custom-call(bf16[512,1024]{1,0:T(8,128)(2,1)} %copy-done.3, bf16[512,1024]{1,0:T(8,128)(2,1)} %collective-permute-done.26.refs_1_, bf16[512,1024]{1,0:T(8,128)(2,1)} %collective-permute-done.27.refs_2_, bf16[128,1152]{1,0:T(8,128)(2,1)} %get-tuple-element.99.refs_1_.refs_3_.refs_2_, ...), custom_call_target="tpu_custom_call" | custom-call | flops 1000000000 | bytes 2097152 | tf_op jit(solution)/shard_map/hidden/pallas_call | solution.py:221
  204.9 4.8 %down.4 = (bf16[128,1024]{1,0:T(8,128)(2,1)S(1)}, bf16[128,1024]{1,0:T(8,128)(2,1)S(1)}, bf16[128,1024]{1,0:T(8,128)(2,1)S(1)}, bf16[128,1024]{1,0:T(8,128)(2,1)S(1)}) custom-call(s32[3]{0:T(128)S(1)} %copy-done.17, bf16[512,512]{1,0:T(8,128)(2,1)} %hidden.1.refs_1_, bf16[128,1152]{1,0:T(8,128)(2,1)S(1)} %copy-done.6, bf16[128,1152]{1,0:T(8,128)(2,1)S(1)} %copy-done.8, ...), custom_call_target="tpu_custom_call" | custom-call | flops 2147483648 | bytes 4194304 | tf_op jit(solution)/shard_map/down/pallas_call | solution.py:270
  212.1 1.8 collective-permute-start.31
  213.9 13.2 %collective-permute-done.32.refs_1_ = bf16[512,512]{1,0:T(8,128)(2,1)S(1)} collective-permute-done((bf16[512,512]{1,0:T(8,128)(2,1)}, bf16[512,512]{1,0:T(8,128)(2,1)S(1)}, u32[]{:S(2)}, u32[]{:S(2)}) %collective-permute-start.32) | collective-permute-done | bytes 524320 | tf_op jit(solution)/shard_map/ppermute | solution.py:346
  227.8 5.4 %down.5 = (bf16[128,1024]{1,0:T(8,128)(2,1)S(1)}, bf16[128,1024]{1,0:T(8,128)(2,1)}, bf16[128,1024]{1,0:T(8,128)(2,1)}, bf16[128,1024]{1,0:T(8,128)(2,1)}) custom-call(s32[3]{0:T(128)S(1)} %copy-done.17, bf16[512,512]{1,0:T(8,128)(2,1)S(1)} %collective-permute-done.32.refs_1_, bf16[128,1152]{1,0:T(8,128)(2,1)S(1)} %copy-done.39, ...), custom_call_target="tpu_custom_call" | custom-call | flops 2147483648 | bytes 4194304 | tf_op jit(solution)/shard_map/down/pallas_call | solution.py:270
  235.6 1.8 collective-permute-start.35
  237.5 2.1 combine.4.refs_1_
  243.6 5.6 %down.6 = (bf16[128,1024]{1,0:T(8,128)(2,1)S(1)}, bf16[128,1024]{1,0:T(8,128)(2,1)}, bf16[128,1024]{1,0:T(8,128)(2,1)}, bf16[128,1024]{1,0:T(8,128)(2,1)}) custom-call(s32[3]{0:T(128)S(1)} %copy-done.18, bf16[512,512]{1,0:T(8,128)(2,1)} %collective-permute-done.36.refs_1_, bf16[128,1152]{1,0:T(8,128)(2,1)S(1)} %copy-done.31, ...), custom_call_target="tpu_custom_call" | custom-call | flops 2147483648 | bytes 4194304 | tf_op jit(solution)/shard_map/down/pallas_call | solution.py:270
  251.6 1.8 collective-permute-start.40
  253.4 2.1 combine.5
  256.5 5.4 %down.7 = (bf16[128,1024]{1,0:T(8,128)(2,1)S(1)}, bf16[128,1024]{1,0:T(8,128)(2,1)}, bf16[128,1024]{1,0:T(8,128)(2,1)}, bf16[128,1024]{1,0:T(8,128)(2,1)}) custom-call(s32[3]{0:T(128)S(1)} %copy-done.19, bf16[512,512]{1,0:T(8,128)(2,1)S(1)} %collective-permute-done.41.refs_1_, bf16[128,1152]{1,0:T(8,128)(2,1)S(1)} %copy-done.23, ...), custom_call_target="tpu_custom_call" | custom-call | flops 2147483648 | bytes 4194304 | tf_op jit(solution)/shard_map/down/pallas_call | solution.py:270
  264.3 1.8 collective-permute-start.45
  266.1 1.7 collective-permute-start.37
  267.8 2.1 combine.6
  270.0 3.4 %collective-permute-start.42 = (bf16[128,1024]{1,0:T(8,128)(2,1)}, bf16[128,1024]{1,0:T(8,128)(2,1)S(1)}, u32[]{:S(2)}, u32[]{:S(2)}) collective-permute-start(bf16[128,1024]{1,0:T(8,128)(2,1)} %combine.6), channel_id=1, source_target_pairs={{0,4},{1,5},{2,6},{3,7},{4,0},{5,1},{6,2},{7,3},{8,12},{9,13},{10,... | collective-permute-start | bytes 786440 | tf_op jit(solution)/shard_map/ppermute | solution.py:346
  275.3 2.1 combine.7
  277.4 3.2 %collective-permute-start.46 = (bf16[128,1024]{1,0:T(8,128)(2,1)}, bf16[128,1024]{1,0:T(8,128)(2,1)S(1)}, u32[]{:S(2)}, u32[]{:S(2)}) collective-permute-start(bf16[128,1024]{1,0:T(8,128)(2,1)} %combine.7), channel_id=1, source_target_pairs={{0,6},{1,7},{2,4},{3,5},{4,2},{5,3},{6,0},{7,1},{8,14},{9,15},{10,... | collective-permute-start | bytes 786440 | tf_op jit(solution)/shard_map/ppermute | solution.py:346
  280.6 7.6 %collective-permute-done.42.refs_3_ = bf16[128,1024]{1,0:T(8,128)(2,1)S(1)} collective-permute-done((bf16[128,1024]{1,0:T(8,128)(2,1)}, bf16[128,1024]{1,0:T(8,128)(2,1)S(1)}, u32[]{:S(2)}, u32[]{:S(2)}) %collective-permute-start.42) | collective-permute-done | bytes 262176 | tf_op jit(solution)/shard_map/ppermute | solution.py:346
  289.7 2.4 place.1
  (201 shorter events, 44.0 us)
Async XLA Ops:
  3.7 27.3 %collective-permute-start.11 = (bf16[8,128,512]{2,1,0:T(8,128)(2,1)}, bf16[8,128,512]{2,1,0:T(8,128)(2,1)}, u32[]{:S(2)}, u32[]{:S(2)}) collective-permute-start(bf16[8,128,512]{2,1,0:T(8,128)(2,1)} %pad_maximum_fusion.3), channel_id=1, source_target_pairs={{0,8},{1,9},{2,10},{3,11},{4,12},{5,13},{6,14},{7,15},{8,0},{9,1},... | collective-permute-start | bytes 3145736 | tf_op jit(solution)/shard_map/ppermute | solution.py:346
  7.8 47.4 %collective-permute-start.12 = (bf16[8,128,512]{2,1,0:T(8,128)(2,1)}, bf16[8,128,512]{2,1,0:T(8,128)(2,1)}, u32[]{:S(2)}, u32[]{:S(2)}) collective-permute-start(bf16[8,128,512]{2,1,0:T(8,128)(2,1)} %pad_maximum_fusion.4), channel_id=1, source_target_pairs={{0,16},{1,17},{2,18},{3,19},{4,20},{5,21},{6,22},{7,23},{8,24},{9,... | collective-permute-start | bytes 3145736 | tf_op jit(solution)/shard_map/ppermute | solution.py:346
  10.4 44.8 %collective-permute-start.13 = (bf16[8,128,512]{2,1,0:T(8,128)(2,1)}, bf16[8,128,512]{2,1,0:T(8,128)(2,1)}, u32[]{:S(2)}, u32[]{:S(2)}) collective-permute-start(bf16[8,128,512]{2,1,0:T(8,128)(2,1)} %pad_maximum_fusion.5), channel_id=1, source_target_pairs={{0,24},{1,25},{2,26},{3,27},{4,28},{5,29},{6,30},{7,31},{8,16},{9,... | collective-permute-start | bytes 3145736 | tf_op jit(solution)/shard_map/ppermute | solution.py:346
  57.4 39.6 %copy-start = (bf16[4,8,128,512]{3,2,1,0:T(8,128)(2,1)}, bf16[4,8,128,512]{3,2,1,0:T(8,128)(2,1)S(1)}, u32[]{:S(2)}) copy-start(bf16[4,8,128,512]{3,2,1,0:T(8,128)(2,1)S(1)} %pad_maximum_fusion.refs_5_) | copy-start | bytes 12582916
  57.4 33.1 %collective-permute-start.14 = (bf16[4,8,128,512]{3,2,1,0:T(8,128)(2,1)S(1)}, bf16[4,8,128,512]{3,2,1,0:T(8,128)(2,1)S(1)}, u32[]{:S(2)}, u32[]{:S(2)}) collective-permute-start(bf16[4,8,128,512]{3,2,1,0:T(8,128)(2,1)S(1)} %pad_maximum_fusion.refs_5_), channel_id=1, source_target_pairs={{0,1},{1,0},{2,3},{3,2},{4,5},{5,4},{6,7},{7,6},{8,9},{9,8},{10,11... | collective-permute-start | bytes 12582920 | tf_op jit(solution)/shard_map/ppermute | solution.py:346
  57.5 11.8 %collective-permute-start.7 = (bf16[128,1152]{1,0:T(8,128)(2,1)S(1)}, bf16[128,1152]{1,0:T(8,128)(2,1)S(1)}, u32[]{:S(2)}, u32[]{:S(2)}) collective-permute-start(bf16[128,1152]{1,0:T(8,128)(2,1)S(1)} %copy-done.63), channel_id=1, source_target_pairs={{0,6},{1,7},{2,4},{3,5},{4,2},{5,3},{6,0},{7,1},{8,14},{9,15},{10,... | collective-permute-start | bytes 884744 | tf_op jit(solution)/shard_map/ppermute | solution.py:346
  61.2 25.7 %collective-permute-start.3 = (bf16[128,1152]{1,0:T(8,128)(2,1)S(1)}, bf16[128,1152]{1,0:T(8,128)(2,1)S(1)}, u32[]{:S(2)}, u32[]{:S(2)}) collective-permute-start(bf16[128,1152]{1,0:T(8,128)(2,1)S(1)} %copy-done.62), channel_id=1, source_target_pairs={{0,4},{1,5},{2,6},{3,7},{4,0},{5,1},{6,2},{7,3},{8,12},{9,13},{10,... | collective-permute-start | bytes 884744 | tf_op jit(solution)/shard_map/ppermute | solution.py:346
  69.4 17.5 %collective-permute-start.10 = (bf16[128,1152]{1,0:T(8,128)(2,1)S(1)}, bf16[128,1152]{1,0:T(8,128)(2,1)S(1)}, u32[]{:S(2)}, u32[]{:S(2)}) collective-permute-start(bf16[128,1152]{1,0:T(8,128)(2,1)S(1)} %collective-permute-done.7.refs_1_.refs_2_), channel_id=1, source_target_pairs={{0,24},{1,25},{2,26},{3,27},{4,28},{5,29},{6,30},{7,31},{8,16},{9,... | collective-permute-start | bytes 884744 | tf_op jit(solution)/shard_map/ppermute | solution.py:346
  70.8 16.7 %collective-permute-start.8 = (bf16[128,1152]{1,0:T(8,128)(2,1)S(1)}, bf16[128,1152]{1,0:T(8,128)(2,1)S(1)}, u32[]{:S(2)}, u32[]{:S(2)}) collective-permute-start(bf16[128,1152]{1,0:T(8,128)(2,1)S(1)} %collective-permute-done.7.refs_1_.refs_2_), channel_id=1, source_target_pairs={{0,8},{1,9},{2,10},{3,11},{4,12},{5,13},{6,14},{7,15},{8,0},{9,1},... | collective-permute-start | bytes 884744 | tf_op jit(solution)/shard_map/ppermute | solution.py:346
  72.3 16.7 %collective-permute-start.9 = (bf16[128,1152]{1,0:T(8,128)(2,1)S(1)}, bf16[128,1152]{1,0:T(8,128)(2,1)S(1)}, u32[]{:S(2)}, u32[]{:S(2)}) collective-permute-start(bf16[128,1152]{1,0:T(8,128)(2,1)S(1)} %collective-permute-done.7.refs_1_.refs_2_), channel_id=1, source_target_pairs={{0,16},{1,17},{2,18},{3,19},{4,20},{5,21},{6,22},{7,23},{8,24},{9,... | collective-permute-start | bytes 884744 | tf_op jit(solution)/shard_map/ppermute | solution.py:346
  86.9 23.4 %collective-permute-start.17 = (bf16[128,1152]{1,0:T(8,128)(2,1)S(1)}, bf16[128,1152]{1,0:T(8,128)(2,1)S(1)}, u32[]{:S(2)}, u32[]{:S(2)}) collective-permute-start(bf16[128,1152]{1,0:T(8,128)(2,1)S(1)} %copy-done.61), channel_id=1, source_target_pairs={{0,2},{1,3},{2,0},{3,1},{4,6},{5,7},{6,4},{7,5},{8,10},{9,11},{10,... | collective-permute-start | bytes 884744 | tf_op jit(solution)/shard_map/ppermute | solution.py:346
  86.9 25.0 %collective-permute-start.4 = (bf16[128,1152]{1,0:T(8,128)(2,1)S(1)}, bf16[128,1152]{1,0:T(8,128)(2,1)S(1)}, u32[]{:S(2)}, u32[]{:S(2)}) collective-permute-start(bf16[128,1152]{1,0:T(8,128)(2,1)S(1)} %collective-permute-done.3.refs_1_.refs_2_), channel_id=1, source_target_pairs={{0,8},{1,9},{2,10},{3,11},{4,12},{5,13},{6,14},{7,15},{8,0},{9,1},... | collective-permute-start | bytes 884744 | tf_op jit(solution)/shard_map/ppermute | solution.py:346
  87.5 25.9 %collective-permute-start.5 = (bf16[128,1152]{1,0:T(8,128)(2,1)S(1)}, bf16[128,1152]{1,0:T(8,128)(2,1)S(1)}, u32[]{:S(2)}, u32[]{:S(2)}) collective-permute-start(bf16[128,1152]{1,0:T(8,128)(2,1)S(1)} %collective-permute-done.3.refs_1_.refs_2_), channel_id=1, source_target_pairs={{0,16},{1,17},{2,18},{3,19},{4,20},{5,21},{6,22},{7,23},{8,24},{9,... | collective-permute-start | bytes 884744 | tf_op jit(solution)/shard_map/ppermute | solution.py:346
  89.0 24.9 %collective-permute-start.6 = (bf16[128,1152]{1,0:T(8,128)(2,1)S(1)}, bf16[128,1152]{1,0:T(8,128)(2,1)S(1)}, u32[]{:S(2)}, u32[]{:S(2)}) collective-permute-start(bf16[128,1152]{1,0:T(8,128)(2,1)S(1)} %collective-permute-done.3.refs_1_.refs_2_), channel_id=1, source_target_pairs={{0,24},{1,25},{2,26},{3,27},{4,28},{5,29},{6,30},{7,31},{8,16},{9,... | collective-permute-start | bytes 884744 | tf_op jit(solution)/shard_map/ppermute | solution.py:346
  97.0 39.3 %collective-permute-start.15 = (bf16[512,1024]{1,0:T(8,128)(2,1)S(1)}, bf16[512,1024]{1,0:T(8,128)(2,1)}, u32[]{:S(2)}, u32[]{:S(2)}) collective-permute-start(bf16[512,1024]{1,0:T(8,128)(2,1)S(1)} %product.4), channel_id=1, source_target_pairs={{0,2},{1,3},{8,10},{9,11},{16,18},{17,19},{24,26},{25,27}} | collective-permute-start | bytes 3145736 | tf_op jit(solution)/shard_map/ppermute | solution.py:346
  110.3 26.0 %collective-permute-start.16 = (bf16[512,1024]{1,0:T(8,128)(2,1)S(1)}, bf16[512,1024]{1,0:T(8,128)(2,1)}, u32[]{:S(2)}, u32[]{:S(2)}) collective-permute-start(bf16[512,1024]{1,0:T(8,128)(2,1)S(1)} %product.4), channel_id=1, source_target_pairs={{6,4},{7,5},{14,12},{15,13},{22,20},{23,21},{30,28},{31,29}} | collective-permute-start | bytes 3145736 | tf_op jit(solution)/shard_map/ppermute | solution.py:346
  111.9 14.3 %collective-permute-start.18 = (bf16[128,1152]{1,0:T(8,128)(2,1)S(1)}, bf16[128,1152]{1,0:T(8,128)(2,1)S(1)}, u32[]{:S(2)}, u32[]{:S(2)}) collective-permute-start(bf16[128,1152]{1,0:T(8,128)(2,1)S(1)} %collective-permute-done.17.refs_1_.refs_2_), channel_id=1, source_target_pairs={{0,8},{1,9},{2,10},{3,11},{4,12},{5,13},{6,14},{7,15},{8,0},{9,1},... | collective-permute-start | bytes 884744 | tf_op jit(solution)/shard_map/ppermute | solution.py:346
  113.4 14.4 %collective-permute-start.19 = (bf16[128,1152]{1,0:T(8,128)(2,1)S(1)}, bf16[128,1152]{1,0:T(8,128)(2,1)S(1)}, u32[]{:S(2)}, u32[]{:S(2)}) collective-permute-start(bf16[128,1152]{1,0:T(8,128)(2,1)S(1)} %collective-permute-done.17.refs_1_.refs_2_), channel_id=1, source_target_pairs={{0,16},{1,17},{2,18},{3,19},{4,20},{5,21},{6,22},{7,23},{8,24},{9,... | collective-permute-start | bytes 884744 | tf_op jit(solution)/shard_map/ppermute | solution.py:346
  114.0 14.4 %collective-permute-start.20 = (bf16[128,1152]{1,0:T(8,128)(2,1)S(1)}, bf16[128,1152]{1,0:T(8,128)(2,1)S(1)}, u32[]{:S(2)}, u32[]{:S(2)}) collective-permute-start(bf16[128,1152]{1,0:T(8,128)(2,1)S(1)} %collective-permute-done.17.refs_1_.refs_2_), channel_id=1, source_target_pairs={{0,24},{1,25},{2,26},{3,27},{4,28},{5,29},{6,30},{7,31},{8,16},{9,... | collective-permute-start | bytes 884744 | tf_op jit(solution)/shard_map/ppermute | solution.py:346
  126.3 17.4 %collective-permute-start = (bf16[128,1152]{1,0:T(8,128)(2,1)S(1)}, bf16[128,1152]{1,0:T(8,128)(2,1)S(1)}, u32[]{:S(2)}, u32[]{:S(2)}) collective-permute-start(bf16[128,1152]{1,0:T(8,128)(2,1)S(1)} %copy-done.5), channel_id=1, source_target_pairs={{0,8},{1,9},{2,10},{3,11},{4,12},{5,13},{6,14},{7,15},{8,0},{9,1},... | collective-permute-start | bytes 884744 | tf_op jit(solution)/shard_map/ppermute | solution.py:346
  127.8 17.4 %collective-permute-start.1 = (bf16[128,1152]{1,0:T(8,128)(2,1)S(1)}, bf16[128,1152]{1,0:T(8,128)(2,1)S(1)}, u32[]{:S(2)}, u32[]{:S(2)}) collective-permute-start(bf16[128,1152]{1,0:T(8,128)(2,1)S(1)} %copy-done.5), channel_id=1, source_target_pairs={{0,16},{1,17},{2,18},{3,19},{4,20},{5,21},{6,22},{7,23},{8,24},{9,... | collective-permute-start | bytes 884744 | tf_op jit(solution)/shard_map/ppermute | solution.py:346
  128.4 17.5 %collective-permute-start.2 = (bf16[128,1152]{1,0:T(8,128)(2,1)S(1)}, bf16[128,1152]{1,0:T(8,128)(2,1)S(1)}, u32[]{:S(2)}, u32[]{:S(2)}) collective-permute-start(bf16[128,1152]{1,0:T(8,128)(2,1)S(1)} %copy-done.5), channel_id=1, source_target_pairs={{0,24},{1,25},{2,26},{3,27},{4,28},{5,29},{6,30},{7,31},{8,16},{9,... | collective-permute-start | bytes 884744 | tf_op jit(solution)/shard_map/ppermute | solution.py:346
  139.6 26.1 %collective-permute-start.21 = (bf16[512,1024]{1,0:T(8,128)(2,1)}, bf16[512,1024]{1,0:T(8,128)(2,1)}, u32[]{:S(2)}, u32[]{:S(2)}) collective-permute-start(bf16[512,1024]{1,0:T(8,128)(2,1)} %add_convert_fusion.2), channel_id=1, source_target_pairs={{0,2},{1,3},{2,4},{3,5},{8,10},{9,11},{10,12},{11,13},{16,18},{17,... | collective-permute-start | bytes 3145736 | tf_op jit(solution)/shard_map/ppermute | solution.py:346
  142.0 23.7 %collective-permute-start.22 = (bf16[512,1024]{1,0:T(8,128)(2,1)}, bf16[512,1024]{1,0:T(8,128)(2,1)}, u32[]{:S(2)}, u32[]{:S(2)}) collective-permute-start(bf16[512,1024]{1,0:T(8,128)(2,1)} %add_convert_fusion.2), channel_id=1, source_target_pairs={{4,2},{5,3},{6,4},{7,5},{12,10},{13,11},{14,12},{15,13},{20,18},{2... | collective-permute-start | bytes 3145736 | tf_op jit(solution)/shard_map/ppermute | solution.py:346
  143.7 14.7 %collective-permute-start.23 = (bf16[8,128,256]{2,1,0:T(8,128)(2,1)S(1)}, bf16[8,128,256]{2,1,0:T(8,128)(2,1)S(1)}, u32[]{:S(2)}, u32[]{:S(2)}) collective-permute-start(bf16[8,128,256]{2,1,0:T(8,128)(2,1)S(1)} %copy-done.50), channel_id=1, source_target_pairs={{0,8},{1,9},{2,10},{3,11},{4,12},{5,13},{6,14},{7,15},{8,0},{9,1},... | collective-permute-start | bytes 1572872 | tf_op jit(solution)/shard_map/ppermute | solution.py:346
  145.2 20.1 %collective-permute-start.24 = (bf16[8,128,256]{2,1,0:T(8,128)(2,1)S(1)}, bf16[8,128,256]{2,1,0:T(8,128)(2,1)S(1)}, u32[]{:S(2)}, u32[]{:S(2)}) collective-permute-start(bf16[8,128,256]{2,1,0:T(8,128)(2,1)S(1)} %copy-done.49), channel_id=1, source_target_pairs={{0,16},{1,17},{2,18},{3,19},{4,20},{5,21},{6,22},{7,23},{8,24},{9,... | collective-permute-start | bytes 1572872 | tf_op jit(solution)/shard_map/ppermute | solution.py:346
  145.8 19.5 %collective-permute-start.25 = (bf16[8,128,256]{2,1,0:T(8,128)(2,1)S(1)}, bf16[8,128,256]{2,1,0:T(8,128)(2,1)S(1)}, u32[]{:S(2)}, u32[]{:S(2)}) collective-permute-start(bf16[8,128,256]{2,1,0:T(8,128)(2,1)S(1)} %copy-done.48), channel_id=1, source_target_pairs={{0,24},{1,25},{2,26},{3,27},{4,28},{5,29},{6,30},{7,31},{8,16},{9,... | collective-permute-start | bytes 1572872 | tf_op jit(solution)/shard_map/ppermute | solution.py:346
  165.6 39.3 %collective-permute-start.28 = (bf16[4,8,128,256]{3,2,1,0:T(8,128)(2,1)S(1)}, bf16[4,8,128,256]{3,2,1,0:T(8,128)(2,1)}, u32[]{:S(2)}, u32[]{:S(2)}) collective-permute-start(bf16[4,8,128,256]{3,2,1,0:T(8,128)(2,1)S(1)} %pad_maximum_fusion.1.refs_6_), channel_id=1, source_target_pairs={{0,1},{1,0},{2,3},{3,2},{4,5},{5,4},{6,7},{7,6},{8,9},{9,8},{10,11... | collective-permute-start | bytes 6291464 | tf_op jit(solution)/shard_map/ppermute | solution.py:346
  168.5 24.6 %collective-permute-start.26 = (bf16[512,1024]{1,0:T(8,128)(2,1)S(1)}, bf16[512,1024]{1,0:T(8,128)(2,1)}, u32[]{:S(2)}, u32[]{:S(2)}) collective-permute-start(bf16[512,1024]{1,0:T(8,128)(2,1)S(1)} %get-tuple-element.148), channel_id=1, source_target_pairs={{0,2},{1,3},{2,4},{3,5},{4,6},{5,7},{8,10},{9,11},{10,12},{11,13},... | collective-permute-start | bytes 3145736 | tf_op jit(solution)/shard_map/ppermute | solution.py:346
  171.0 27.5 %collective-permute-start.27 = (bf16[512,1024]{1,0:T(8,128)(2,1)S(1)}, bf16[512,1024]{1,0:T(8,128)(2,1)}, u32[]{:S(2)}, u32[]{:S(2)}) collective-permute-start(bf16[512,1024]{1,0:T(8,128)(2,1)S(1)} %get-tuple-element.147), channel_id=1, source_target_pairs={{2,0},{3,1},{4,2},{5,3},{6,4},{7,5},{10,8},{11,9},{12,10},{13,11},... | collective-permute-start | bytes 3145736 | tf_op jit(solution)/shard_map/ppermute | solution.py:346
  202.3 24.8 %collective-permute-start.32 = (bf16[512,512]{1,0:T(8,128)(2,1)}, bf16[512,512]{1,0:T(8,128)(2,1)S(1)}, u32[]{:S(2)}, u32[]{:S(2)}) collective-permute-start(bf16[512,512]{1,0:T(8,128)(2,1)} %hidden.1.refs_1_), channel_id=1, source_target_pairs={{0,2},{1,3},{2,0},{3,1},{4,6},{5,7},{6,4},{7,5},{8,10},{9,11},{10,... | collective-permute-start | bytes 1572872 | tf_op jit(solution)/shard_map/ppermute | solution.py:346
  203.7 35.9 %collective-permute-start.36 = (bf16[512,512]{1,0:T(8,128)(2,1)}, bf16[512,512]{1,0:T(8,128)(2,1)}, u32[]{:S(2)}, u32[]{:S(2)}) collective-permute-start(bf16[512,512]{1,0:T(8,128)(2,1)} %hidden.1.refs_1_), channel_id=1, source_target_pairs={{0,4},{1,5},{2,6},{3,7},{4,0},{5,1},{6,2},{7,3},{8,12},{9,13},{10,... | collective-permute-start | bytes 1572872 | tf_op jit(solution)/shard_map/ppermute | solution.py:346
  210.4 23.5 %collective-permute-start.29 = (bf16[128,1024]{1,0:T(8,128)(2,1)S(1)}, bf16[128,1024]{1,0:T(8,128)(2,1)S(1)}, u32[]{:S(2)}, u32[]{:S(2)}) collective-permute-start(bf16[128,1024]{1,0:T(8,128)(2,1)S(1)} %get-tuple-element.113), channel_id=1, source_target_pairs={{0,8},{1,9},{2,10},{3,11},{4,12},{5,13},{6,14},{7,15},{8,0},{9,1},... | collective-permute-start | bytes 786440 | tf_op jit(solution)/shard_map/ppermute | solution.py:346
  211.0 23.5 %collective-permute-start.30 = (bf16[128,1024]{1,0:T(8,128)(2,1)S(1)}, bf16[128,1024]{1,0:T(8,128)(2,1)S(1)}, u32[]{:S(2)}, u32[]{:S(2)}) collective-permute-start(bf16[128,1024]{1,0:T(8,128)(2,1)S(1)} %get-tuple-element.114), channel_id=1, source_target_pairs={{0,16},{1,17},{2,18},{3,19},{4,20},{5,21},{6,22},{7,23},{8,24},{9,... | collective-permute-start | bytes 786440 | tf_op jit(solution)/shard_map/ppermute | solution.py:346
  212.1 23.6 %collective-permute-start.31 = (bf16[128,1024]{1,0:T(8,128)(2,1)S(1)}, bf16[128,1024]{1,0:T(8,128)(2,1)S(1)}, u32[]{:S(2)}, u32[]{:S(2)}) collective-permute-start(bf16[128,1024]{1,0:T(8,128)(2,1)S(1)} %get-tuple-element.115), channel_id=1, source_target_pairs={{0,24},{1,25},{2,26},{3,27},{4,28},{5,29},{6,30},{7,31},{8,16},{9,... | collective-permute-start | bytes 786440 | tf_op jit(solution)/shard_map/ppermute | solution.py:346
  227.1 28.4 %collective-permute-start.41 = (bf16[512,512]{1,0:T(8,128)(2,1)}, bf16[512,512]{1,0:T(8,128)(2,1)S(1)}, u32[]{:S(2)}, u32[]{:S(2)}) collective-permute-start(bf16[512,512]{1,0:T(8,128)(2,1)} %hidden.1.refs_1_), channel_id=1, source_target_pairs={{0,6},{1,7},{2,4},{3,5},{4,2},{5,3},{6,0},{7,1},{8,14},{9,15},{10,... | collective-permute-start | bytes 1572872 | tf_op jit(solution)/shard_map/ppermute | solution.py:346
  234.0 16.5 %collective-permute-start.33 = (bf16[128,1024]{1,0:T(8,128)(2,1)}, bf16[128,1024]{1,0:T(8,128)(2,1)}, u32[]{:S(2)}, u32[]{:S(2)}) collective-permute-start(bf16[128,1024]{1,0:T(8,128)(2,1)} %get-tuple-element.118), channel_id=1, source_target_pairs={{0,8},{1,9},{2,10},{3,11},{4,12},{5,13},{6,14},{7,15},{8,0},{9,1},... | collective-permute-start | bytes 786440 | tf_op jit(solution)/shard_map/ppermute | solution.py:346
  234.5 17.0 %collective-permute-start.34 = (bf16[128,1024]{1,0:T(8,128)(2,1)}, bf16[128,1024]{1,0:T(8,128)(2,1)}, u32[]{:S(2)}, u32[]{:S(2)}) collective-permute-start(bf16[128,1024]{1,0:T(8,128)(2,1)} %get-tuple-element.119), channel_id=1, source_target_pairs={{0,16},{1,17},{2,18},{3,19},{4,20},{5,21},{6,22},{7,23},{8,24},{9,... | collective-permute-start | bytes 786440 | tf_op jit(solution)/shard_map/ppermute | solution.py:346
  235.6 17.7 %collective-permute-start.35 = (bf16[128,1024]{1,0:T(8,128)(2,1)}, bf16[128,1024]{1,0:T(8,128)(2,1)}, u32[]{:S(2)}, u32[]{:S(2)}) collective-permute-start(bf16[128,1024]{1,0:T(8,128)(2,1)} %get-tuple-element.120), channel_id=1, source_target_pairs={{0,24},{1,25},{2,26},{3,27},{4,28},{5,29},{6,30},{7,31},{8,16},{9,... | collective-permute-start | bytes 786440 | tf_op jit(solution)/shard_map/ppermute | solution.py:346
  249.9 14.4 %collective-permute-start.38 = (bf16[128,1024]{1,0:T(8,128)(2,1)}, bf16[128,1024]{1,0:T(8,128)(2,1)}, u32[]{:S(2)}, u32[]{:S(2)}) collective-permute-start(bf16[128,1024]{1,0:T(8,128)(2,1)} %get-tuple-element.127), channel_id=1, source_target_pairs={{0,8},{1,9},{2,10},{3,11},{4,12},{5,13},{6,14},{7,15},{8,0},{9,1},... | collective-permute-start | bytes 786440 | tf_op jit(solution)/shard_map/ppermute | solution.py:346
  250.4 15.7 %collective-permute-start.39 = (bf16[128,1024]{1,0:T(8,128)(2,1)}, bf16[128,1024]{1,0:T(8,128)(2,1)}, u32[]{:S(2)}, u32[]{:S(2)}) collective-permute-start(bf16[128,1024]{1,0:T(8,128)(2,1)} %get-tuple-element.128), channel_id=1, source_target_pairs={{0,16},{1,17},{2,18},{3,19},{4,20},{5,21},{6,22},{7,23},{8,24},{9,... | collective-permute-start | bytes 786440 | tf_op jit(solution)/shard_map/ppermute | solution.py:346
  251.6 16.3 %collective-permute-start.40 = (bf16[128,1024]{1,0:T(8,128)(2,1)}, bf16[128,1024]{1,0:T(8,128)(2,1)}, u32[]{:S(2)}, u32[]{:S(2)}) collective-permute-start(bf16[128,1024]{1,0:T(8,128)(2,1)} %get-tuple-element.129), channel_id=1, source_target_pairs={{0,24},{1,25},{2,26},{3,27},{4,28},{5,29},{6,30},{7,31},{8,16},{9,... | collective-permute-start | bytes 786440 | tf_op jit(solution)/shard_map/ppermute | solution.py:346
  262.6 10.7 %collective-permute-start.43 = (bf16[128,1024]{1,0:T(8,128)(2,1)}, bf16[128,1024]{1,0:T(8,128)(2,1)S(1)}, u32[]{:S(2)}, u32[]{:S(2)}) collective-permute-start(bf16[128,1024]{1,0:T(8,128)(2,1)} %get-tuple-element.136), channel_id=1, source_target_pairs={{0,8},{1,9},{2,10},{3,11},{4,12},{5,13},{6,14},{7,15},{8,0},{9,1},... | collective-permute-start | bytes 786440 | tf_op jit(solution)/shard_map/ppermute | solution.py:346
  263.2 10.7 %collective-permute-start.44 = (bf16[128,1024]{1,0:T(8,128)(2,1)}, bf16[128,1024]{1,0:T(8,128)(2,1)S(1)}, u32[]{:S(2)}, u32[]{:S(2)}) collective-permute-start(bf16[128,1024]{1,0:T(8,128)(2,1)} %get-tuple-element.137), channel_id=1, source_target_pairs={{0,16},{1,17},{2,18},{3,19},{4,20},{5,21},{6,22},{7,23},{8,24},{9,... | collective-permute-start | bytes 786440 | tf_op jit(solution)/shard_map/ppermute | solution.py:346
  264.3 9.6 %collective-permute-start.45 = (bf16[128,1024]{1,0:T(8,128)(2,1)}, bf16[128,1024]{1,0:T(8,128)(2,1)S(1)}, u32[]{:S(2)}, u32[]{:S(2)}) collective-permute-start(bf16[128,1024]{1,0:T(8,128)(2,1)} %get-tuple-element.138), channel_id=1, source_target_pairs={{0,24},{1,25},{2,26},{3,27},{4,28},{5,29},{6,30},{7,31},{8,16},{9,... | collective-permute-start | bytes 786440 | tf_op jit(solution)/shard_map/ppermute | solution.py:346
  266.1 22.1 %collective-permute-start.37 = (bf16[128,1024]{1,0:T(8,128)(2,1)}, bf16[128,1024]{1,0:T(8,128)(2,1)S(1)}, u32[]{:S(2)}, u32[]{:S(2)}) collective-permute-start(bf16[128,1024]{1,0:T(8,128)(2,1)} %combine.5), channel_id=1, source_target_pairs={{0,2},{1,3},{2,0},{3,1},{4,6},{5,7},{6,4},{7,5},{8,10},{9,11},{10,... | collective-permute-start | bytes 786440 | tf_op jit(solution)/shard_map/ppermute | solution.py:346
  270.0 18.2 %collective-permute-start.42 = (bf16[128,1024]{1,0:T(8,128)(2,1)}, bf16[128,1024]{1,0:T(8,128)(2,1)S(1)}, u32[]{:S(2)}, u32[]{:S(2)}) collective-permute-start(bf16[128,1024]{1,0:T(8,128)(2,1)} %combine.6), channel_id=1, source_target_pairs={{0,4},{1,5},{2,6},{3,7},{4,0},{5,1},{6,2},{7,3},{8,12},{9,13},{10,... | collective-permute-start | bytes 786440 | tf_op jit(solution)/shard_map/ppermute | solution.py:346
  277.4 10.8 %collective-permute-start.46 = (bf16[128,1024]{1,0:T(8,128)(2,1)}, bf16[128,1024]{1,0:T(8,128)(2,1)S(1)}, u32[]{:S(2)}, u32[]{:S(2)}) collective-permute-start(bf16[128,1024]{1,0:T(8,128)(2,1)} %combine.7), channel_id=1, source_target_pairs={{0,6},{1,7},{2,4},{3,5},{4,2},{5,3},{6,0},{7,1},{8,14},{9,15},{10,... | collective-permute-start | bytes 786440 | tf_op jit(solution)/shard_map/ppermute | solution.py:346
  (63 other events, 727.2 us)
where the time goes:
time: 293 us; the launch traced here: 292 us
  waiting for transfers between devices  120 us (41%)
  starting transfers between devices  74.4 us (25%)
  Pallas kernels  64.9 us (22%)
  local copies, waits for them, and re-layouts  20 us (7%)
  other arithmetic  12.5 us (4%)
    ppermute x47, waiting for transfers between devices, permute(): return lax.ppermute(value, AXES, pairs)  120 us
    ppermute x47, starting transfers between devices, permute(): return lax.ppermute(value, AXES, pairs)  74.4 us
    pallas_call x4, Pallas kernels, expert_product(): pl.pallas_call(lambda *refs: product_kernel(groups, *refs), in_specs=[pl....  25.6 us
    pallas_call x4, Pallas kernels, down_product(): pl.pallas_call(lambda *refs: down_kernel(groups, experts, len(hiddens), *...  21.3 us
    unnamed x129, local copies, waits for them, and re-layouts  15.9 us
    pallas_call x4, Pallas kernels, combine(): pl.pallas_call(lambda *refs: combine_kernel(len(parts), planes, *refs), i...  8.45 us
    convert_element_type x2, other arithmetic, add(): (first.astype(jnp.float32) + second.astype(jnp.float32)).astype(jnp.bfloa...  6.1 us
  transfers between devices with their start and end apart: 47, of which 11 were waited for; matrix products, arithmetic and copies ran while one was open for 4% of the time, Pallas kernels for 21%

commit v1 on v0

--- a/solution.py
+++ b/solution.py
@@ -136,7 +136,8 @@
 
 
 def product_kernel(groups, here, *refs):
-    blocks, (first, second), outs, x_ref = refs[:groups], refs[groups : groups + 2], refs[groups + 2 : -1], refs[-1]
+    blocks, (first, second), outs = refs[:groups], refs[groups : groups + 2], refs[groups + 2 : -2]
+    info_ref, x_ref = refs[-2:]
     experts, hid = first.shape[1], first.shape[-1]
     each = groups // len(outs)
     tile = blocks[0].shape[0]
@@ -149,6 +150,7 @@
                 start = pl.multiple_of((side * groups + (here[0] ^ m)) * LANES, LANES)
                 to = (side * groups + m) * LANES
                 x_ref[at, to : to + LANES] = block[:, pl.ds(start, LANES)]
+        info_ref[at, :] = block[:, depth:]
     routes = [[block[:, depth + k : depth + k + 1].astype(jnp.float32) for k in range(2)] for block in blocks]
 
     def expert(e, carry):
@@ -180,8 +182,9 @@
     return pl.pallas_call(
         lambda *refs: product_kernel(groups, *refs),
         in_specs=[pl.BlockSpec(memory_space=pltpu.SMEM)] + [vmem] * (groups + 2),
-        out_specs=[vmem] * PIECES,
-        out_shape=[jax.ShapeDtypeStruct((tokens // PIECES, 2 * hid), jnp.bfloat16)] * PIECES,
+        out_specs=[vmem] * (PIECES + 1),
+        out_shape=[jax.ShapeDtypeStruct((tokens // PIECES, 2 * hid), jnp.bfloat16)] * PIECES
+        + [jax.ShapeDtypeStruct((tokens, LANES), jnp.bfloat16)],
         scratch_shapes=[pltpu.VMEM((tokens, depth), jnp.bfloat16)],
         cost_estimate=pl.CostEstimate(
             flops=experts * 2 * tokens * depth * hid, transcendentals=0, bytes_accessed=4 * weights[0].size
@@ -192,16 +195,16 @@
 
 
 def hidden_kernel(groups, count, *refs):
-    pieces, blocks, out_ref = refs[: count * PIECES], refs[count * PIECES : -1], refs[-1]
+    pieces, info_ref, out_ref = refs[: count * PIECES], refs[-2], refs[-1]
     each = groups // PIECES
     hid = out_ref.shape[1] // 2
-    tile, lanes = blocks[0].shape
-    depth = lanes - LANES
-    for i, block in enumerate(blocks):
+    tile = info_ref.shape[0] // groups
+    for i in range(groups):
         at = slice(i % each * tile, (i % each + 1) * tile)
+        info = info_ref[i * tile : (i + 1) * tile, :].astype(jnp.float32)
         parts = pieces[i // each :: PIECES]
         for k in range(2):
-            score = [block[:, depth + 2 + 2 * k + n : depth + 3 + 2 * k + n].astype(jnp.float32) for n in range(2)]
+            score = [info[:, 2 + 2 * k + n : 3 + 2 * k + n] for n in range(2)]
             sums = []
             for part in range(2):
                 to = slice((2 * k + part) * hid, (2 * k + part + 1) * hid)
@@ -213,33 +216,31 @@
             out_ref[i * tile : (i + 1) * tile, k * hid : (k + 1) * hid] = value.astype(jnp.bfloat16)
 
 
-def hidden_rows(parts, blocks):
-    groups = len(blocks)
+def hidden_rows(parts, info, groups):
     tokens, columns = parts[0][0].shape[0] * PIECES, parts[0][0].shape[1]
     flat = [piece for part in parts for piece in part]
     vmem = pl.BlockSpec(memory_space=pltpu.VMEM)
     return pl.pallas_call(
         lambda *refs: hidden_kernel(groups, len(parts), *refs),
-        in_specs=[vmem] * (len(flat) + groups),
+        in_specs=[vmem] * (len(flat) + 1),
         out_specs=vmem,
         out_shape=jax.ShapeDtypeStruct((tokens, columns // 2), jnp.bfloat16),
         cost_estimate=pl.CostEstimate(flops=10**9, transcendentals=0, bytes_accessed=4 * tokens * columns),
         name="hidden",
-    )(*flat, *blocks)
+    )(*flat, info)
 
 
 def down_kernel(groups, experts, halves, here, *refs):
-    hiddens, blocks, refs = refs[:halves], refs[halves : halves + groups], refs[halves + groups :]
+    hiddens, info_ref, refs = refs[:halves], refs[halves], refs[halves + 1 :]
     down_a, down_b, outs, wide_ref = refs[0], refs[1], refs[2 : 2 + groups], refs[-1]
     part = hiddens[0].shape[1] // 2
     hid = part * halves
-    tile, lanes = blocks[0].shape
-    depth = lanes - LANES
+    tile = info_ref.shape[0] // groups
     pair = 2 if groups % 2 == 0 else 1
     zero = jnp.zeros((), jnp.float32)
-    for i, block in enumerate(blocks):
+    for i in range(groups):
         at = slice(i * tile, (i + 1) * tile)
-        routes = [block[:, depth + k : depth + k + 1].astype(jnp.float32) for k in range(2)]
+        routes = [info_ref[at, k : k + 1].astype(jnp.float32) for k in range(2)]
         for h, ref in enumerate(hiddens):
             rows = [ref[at, k * part : (k + 1) * part].astype(jnp.float32) for k in range(2)]
             for e in range(experts):
@@ -261,15 +262,15 @@
                     out[:, pl.ds(start, LANES)] = product[i * tile : (i + 1) * tile, p * LANES : (p + 1) * LANES]
 
 
-def down_product(here, hiddens, blocks, down):
-    groups, experts, _, hid = down[0].shape
-    tile, lanes = blocks[0].shape
-    tokens = groups * tile
-    width = lanes - LANES
+def down_product(here, hiddens, info, down):
+    groups, experts, rows, hid = down[0].shape
+    tokens = info.shape[0]
+    tile = tokens // groups
+    width = CORES * groups * rows
     vmem = pl.BlockSpec(memory_space=pltpu.VMEM)
     return pl.pallas_call(
         lambda *refs: down_kernel(groups, experts, len(hiddens), *refs),
-        in_specs=[pl.BlockSpec(memory_space=pltpu.SMEM)] + [vmem] * (len(hiddens) + groups + 2),
+        in_specs=[pl.BlockSpec(memory_space=pltpu.SMEM)] + [vmem] * (len(hiddens) + 3),
         out_specs=[vmem] * groups,
         out_shape=[jax.ShapeDtypeStruct((tile, width), jnp.bfloat16)] * groups,
         scratch_shapes=[pltpu.VMEM((tokens, experts * hid), jnp.bfloat16)],
@@ -278,7 +279,7 @@
         ),
         compiler_params=pltpu.CompilerParams(vmem_limit_bytes=24 * 2**20),
         name="down",
-    )(here, *hiddens, *blocks, *down)
+    )(here, *hiddens, info, *down)
 
 
 def combine_kernel(groups, planes, here, gate_ref, *refs):
@@ -419,8 +420,11 @@
             full = jnp.stack(after(parts, done))
             return full, (full, swap(full))
 
+        infos = {}
+
         def multiply(m, weights, done):
-            return expert_product(here, after(blocks[m], done), weights)
+            *pieces, infos[m] = expert_product(here, after(blocks[m], done), weights)
+            return pieces
 
         def moved(s, partial, arrived, done):
             climb = {p: p ^ (planes - s + p) for p in range(0, s)}
@@ -428,7 +432,11 @@
             news = []
             for r in range(PIECES):
                 mine = {m: pieces[r] for m, pieces in partial.items()}
-                below, above = after(arrived[r], done) if arrived is not None else (None, None)
+                below = above = None
+                if arrived is not None and arrived[r][0] is arrived[r][1]:
+                    below = above = after(arrived[r][0], done)
+                elif arrived is not None:
+                    below, above = after(arrived[r], done)
                 if set(climb) & set(sink):
                     rising, falling = pick(mine, climb), pick(mine, sink)
                     if below is not None:
@@ -436,10 +444,18 @@
                 else:
                     rising = pick(mine, {**climb, **sink})
                     if below is not None:
-                        rising = add(rising, jnp.where(among(climb), below, above))
+                        rising = add(rising, below if below is above else jnp.where(among(climb), below, above))
                     falling = rising
                 done = (rising, falling)
-                news.append((upward(rising, set(climb)), downward(falling, set(sink))))
+                apart = not {p + 1 for p in climb} & {p - 1 for p in sink} and not set(climb) & set(sink)
+                if apart:
+                    both = permute(
+                        rising,
+                        lambda g, z, c: (g, z + 1, c) if z in climb else (g, z - 1, c) if z in sink else None,
+                    )
+                    news.append((both, both))
+                else:
+                    news.append((upward(rising, set(climb)), downward(falling, set(sink))))
             return news, done
 
         last, weights = stack(parts0, cut2)
@@ -457,7 +473,7 @@
             sums, last = moved(far, partial, sums, last)
         arrived = after(sums, last)
         belows, aboves = [one[0] for one in arrived], [one[1] for one in arrived]
-        hidden = hidden_rows([partial[0], belows, aboves], blocks[0])
+        hidden = hidden_rows([partial[0], belows, aboves], infos[0], groups)
         last = hidden
         rows_in = {0: hidden}
         for m in order[:-1]:
@@ -472,12 +488,12 @@
 
         waiting = []
         for m in range(planes):
-            last = out = down_product(here, after([rows_in[m]], last), blocks[m], down_full)
+            last = out = down_product(here, after([rows_in[m]], last), infos[m], down_full)
             parts[m] = [out[0]] + [across(out[b], b) for b in range(1, groups)]
-            if waiting:
+            if waiting and m == 1:
                 last = finish(waiting.pop(0), last)
             waiting.append(m)
-        for m in waiting:
+        for m in waiting[1:-1] + waiting[:1] + waiting[-1:]:
             last = finish(m, last)
         return place(here, [finished[m] for m in range(planes)], groups)
 

time: 293 us -> 309 us (1.055)
  waiting for transfers between devices: 120 us -> 151 us
  local copies, waits for them, and re-layouts: 20 us -> 12.7 us
  starting transfers between devices: 74.4 us -> 70.7 us
    ppermute x47 -> x46, waiting for transfers between devices: 120 us -> 151 us  [permute(): return lax.ppermute(value, AXES, pairs)]
    unnamed x129 -> x77, local copies, waits for them, and re-layouts: 15.9 us -> 9.83 us
    ppermute x47 -> x46, starting transfers between devices: 74.4 us -> 70.7 us  [permute(): return lax.ppermute(value, AXES, pairs)]
  transfers between devices with their start and end apart: 47 -> 46, of which waited for: 11 -> 21; matrix products, arithmetic and copies ran while one was open for 4% -> 3% of each run, Pallas kernels for 21% -> 19%
where the time goes in v1:
time: 309 us; the launch traced here: 308 us
  waiting for transfers between devices  151 us (49%)
  starting transfers between devices  70.7 us (23%)
  Pallas kernels  63 us (20%)
  local copies, waits for them, and re-layouts  12.7 us (4%)
  other arithmetic  10.6 us (3%)
    ppermute x46, waiting for transfers between devices, permute(): return lax.ppermute(value, AXES, pairs)  151 us
    ppermute x46, starting transfers between devices, permute(): return lax.ppermute(value, AXES, pairs)  70.7 us
    pallas_call x4, Pallas kernels, expert_product(): pl.pallas_call(lambda *refs: product_kernel(groups, *refs), in_specs=[pl....  25.8 us
    pallas_call x4, Pallas kernels, down_product(): pl.pallas_call(lambda *refs: down_kernel(groups, experts, len(hiddens), *...  19.7 us
    unnamed x77, local copies, waits for them, and re-layouts  9.83 us
    pallas_call x4, Pallas kernels, combine(): pl.pallas_call(lambda *refs: combine_kernel(len(parts), planes, *refs), i...  8.42 us
  transfers between devices with their start and end apart: 46, of which 21 were waited for; matrix products, arithmetic and copies ran while one was open for 3% of the time, Pallas kernels for 19%

profile of v1, /device:TPU:0, one launch (start us, length us, event | category | flops | bytes accessed | tf_op | source)
XLA Modules:
  0.0 308.2 jit_solution(13271023899415010673)
XLA Ops:
  0.0 2.6 constant_dynamic-slice_fusion.4
  3.7 3.0 collective-permute-start.11
  11.7 3.3 %prep.1 = (bf16[128,1152]{1,0:T(8,128)(2,1)}, bf16[128,1152]{1,0:T(8,128)(2,1)}, bf16[128,1152]{1,0:T(8,128)(2,1)}, bf16[128,1152]{1,0:T(8,128)(2,1)}) custom-call(s32[3]{0:T(128)} %pad_add_fusion.here.refs_0_, bf16[128,4096]{1,0:T(8,128)(2,1)} %tok_ref.1, s32[128,2]{1,0:T(8,128)} %copy.10.routes_ref, bf16[8,4096]{1,0:T(8,128)(2,1)} %bitcast.17, ...), custom_call_target="tpu_custom_call" | custom-call | tf_op jit(solution)/shard_map/prep/pallas_call | solution.py:128
  15.4 15.7 %collective-permute-done.11 = bf16[8,128,512]{2,1,0:T(8,128)(2,1)} collective-permute-done((bf16[8,128,512]{2,1,0:T(8,128)(2,1)}, bf16[8,128,512]{2,1,0:T(8,128)(2,1)}, u32[]{:S(2)}, u32[]{:S(2)}) %collective-permute-start.11) | collective-permute-done | bytes 1048608 | tf_op jit(solution)/shard_map/ppermute | solution.py:347
  31.0 24.2 %collective-permute-done.12 = bf16[8,128,512]{2,1,0:T(8,128)(2,1)} collective-permute-done((bf16[8,128,512]{2,1,0:T(8,128)(2,1)}, bf16[8,128,512]{2,1,0:T(8,128)(2,1)}, u32[]{:S(2)}, u32[]{:S(2)}) %collective-permute-start.12) | collective-permute-done | bytes 1048608 | tf_op jit(solution)/shard_map/ppermute | solution.py:347
  55.2 2.2 pad_maximum_fusion.refs_5_
  57.5 3.7 %collective-permute-start.7 = (bf16[128,1152]{1,0:T(8,128)(2,1)S(1)}, bf16[128,1152]{1,0:T(8,128)(2,1)S(1)}, u32[]{:S(2)}, u32[]{:S(2)}) collective-permute-start(bf16[128,1152]{1,0:T(8,128)(2,1)S(1)} %copy-done.37), channel_id=1, source_target_pairs={{0,6},{1,7},{2,4},{3,5},{4,2},{5,3},{6,0},{7,1},{8,14},{9,15},{10,... | collective-permute-start | bytes 884744 | tf_op jit(solution)/shard_map/ppermute | solution.py:347
  61.2 8.2 %collective-permute-done.7.refs_1_ = bf16[128,1152]{1,0:T(8,128)(2,1)S(1)} collective-permute-done((bf16[128,1152]{1,0:T(8,128)(2,1)S(1)}, bf16[128,1152]{1,0:T(8,128)(2,1)S(1)}, u32[]{:S(2)}, u32[]{:S(2)}) %collective-permute-start.7) | collective-permute-done | bytes 294944 | tf_op jit(solution)/shard_map/ppermute | solution.py:347
  72.9 14.0 %collective-permute-done.3.refs_1_ = bf16[128,1152]{1,0:T(8,128)(2,1)S(1)} collective-permute-done((bf16[128,1152]{1,0:T(8,128)(2,1)S(1)}, bf16[128,1152]{1,0:T(8,128)(2,1)S(1)}, u32[]{:S(2)}, u32[]{:S(2)}) %collective-permute-start.3) | collective-permute-done | bytes 294944 | tf_op jit(solution)/shard_map/ppermute | solution.py:347
  90.5 6.5 %product.4 = (bf16[512,1024]{1,0:T(8,128)(2,1)S(1)}, bf16[512,128]{1,0:T(8,128)(2,1)S(1)}) custom-call(s32[3]{0:T(128)S(1)} %copy-done.8, bf16[128,1152]{1,0:T(8,128)(2,1)S(1)} %collective-permute-done.7.refs_1_, bf16[128,1152]{1,0:T(8,128)(2,1)S(1)} %collective-permute-done.8.refs_2_, bf16[128,1152]{1,0:T(8,128)(2,1)S(1)} %collective-permute-done.9.refs_3_, ...), custom_call_target="tpu_custom_call" | custom-call | flops 4294967296 | bytes 8388608 | tf_op jit(solution)/shard_map/product/pallas_call | solution.py:182
  97.0 12.4 %collective-permute-start.15 = (bf16[512,1024]{1,0:T(8,128)(2,1)S(1)}, bf16[512,1024]{1,0:T(8,128)(2,1)S(1)}, u32[]{:S(2)}, u32[]{:S(2)}) collective-permute-start(bf16[512,1024]{1,0:T(8,128)(2,1)S(1)} %get-tuple-element.96), channel_id=1, source_target_pairs={{0,2},{1,3},{6,4},{7,5},{8,10},{9,11},{14,12},{15,13},{16,18},{17,... | collective-permute-start | bytes 3145736 | tf_op jit(solution)/shard_map/ppermute | solution.py:347
  112.0 2.5 collective-permute-start.19
  114.5 6.4 %product.5 = (bf16[512,1024]{1,0:T(8,128)(2,1)S(1)}, bf16[512,128]{1,0:T(8,128)(2,1)S(1)}) custom-call(s32[3]{0:T(128)S(1)} %copy-done.8, bf16[128,1152]{1,0:T(8,128)(2,1)S(1)} %collective-permute-done.3.refs_1_, bf16[128,1152]{1,0:T(8,128)(2,1)S(1)} %collective-permute-done.4.refs_2_, bf16[128,1152]{1,0:T(8,128)(2,1)S(1)} %collective-permute-done.5.refs_3_, ...), custom_call_target="tpu_custom_call" | custom-call | flops 4294967296 | bytes 8388608 | tf_op jit(solution)/shard_map/product/pallas_call | solution.py:182
  120.9 4.8 %collective-permute-done.17.refs_2_ = bf16[128,1152]{1,0:T(8,128)(2,1)S(1)} collective-permute-done((bf16[128,1152]{1,0:T(8,128)(2,1)S(1)}, bf16[128,1152]{1,0:T(8,128)(2,1)S(1)}, u32[]{:S(2)}, u32[]{:S(2)}) %collective-permute-start.17) | collective-permute-done | bytes 294944 | tf_op jit(solution)/shard_map/ppermute | solution.py:347
  126.2 2.5 collective-permute-start.2
  128.6 2.5 collective-permute-done.19.refs_4_
  131.1 6.4 %product.6 = (bf16[512,1024]{1,0:T(8,128)(2,1)S(1)}, bf16[512,128]{1,0:T(8,128)(2,1)S(1)}) custom-call(s32[3]{0:T(128)S(1)} %copy-done.8, bf16[128,1152]{1,0:T(8,128)(2,1)S(1)} %collective-permute-done.16.refs_1_, bf16[128,1152]{1,0:T(8,128)(2,1)S(1)} %collective-permute-done.17.refs_2_, bf16[128,1152]{1,0:T(8,128)(2,1)S(1)} %collective-permute-done.18.refs_3_, ...), custom_call_target="tpu_custom_call" | custom-call | flops 4294967296 | bytes 8388608 | tf_op jit(solution)/shard_map/product/pallas_call | solution.py:182
  139.0 3.1 %collective-permute-start.20 = (bf16[512,1024]{1,0:T(8,128)(2,1)}, bf16[512,1024]{1,0:T(8,128)(2,1)}, u32[]{:S(2)}, u32[]{:S(2)}) collective-permute-start(bf16[512,1024]{1,0:T(8,128)(2,1)} %add_convert_fusion.2), channel_id=1, source_target_pairs={{0,2},{1,3},{2,4},{3,5},{8,10},{9,11},{10,12},{11,13},{16,18},{17,... | collective-permute-start | bytes 3145736 | tf_op jit(solution)/shard_map/ppermute | solution.py:347
  142.1 1.7 collective-permute-start.21
  147.3 6.4 %product.7 = (bf16[512,1024]{1,0:T(8,128)(2,1)S(1)}, bf16[512,128]{1,0:T(8,128)(2,1)S(1)}) custom-call(s32[3]{0:T(128)S(1)} %copy-done.8, bf16[128,1152]{1,0:T(8,128)(2,1)S(1)} %copy-done.10, bf16[128,1152]{1,0:T(8,128)(2,1)S(1)} %collective-permute-done.refs_2_, bf16[128,1152]{1,0:T(8,128)(2,1)S(1)} %collective-permute-done.1.refs_3_, ...), custom_call_target="tpu_custom_call" | custom-call | flops 4294967296 | bytes 8388608 | tf_op jit(solution)/shard_map/product/pallas_call | solution.py:182
  153.7 3.8 %collective-permute-done.22 = bf16[8,128,256]{2,1,0:T(8,128)(2,1)S(1)} collective-permute-done((bf16[8,128,256]{2,1,0:T(8,128)(2,1)S(1)}, bf16[8,128,256]{2,1,0:T(8,128)(2,1)S(1)}, u32[]{:S(2)}, u32[]{:S(2)}) %collective-permute-start.22) | collective-permute-done | bytes 524320 | tf_op jit(solution)/shard_map/ppermute | solution.py:347
  157.6 5.1 %collective-permute-done.23 = bf16[8,128,256]{2,1,0:T(8,128)(2,1)S(1)} collective-permute-done((bf16[8,128,256]{2,1,0:T(8,128)(2,1)S(1)}, bf16[8,128,256]{2,1,0:T(8,128)(2,1)S(1)}, u32[]{:S(2)}, u32[]{:S(2)}) %collective-permute-start.23) | collective-permute-done | bytes 524320 | tf_op jit(solution)/shard_map/ppermute | solution.py:347
  164.5 2.8 add_convert_fusion
  167.4 2.5 collective-permute-start.25
  171.2 21.7 %collective-permute-done.25.refs_1_ = bf16[512,1024]{1,0:T(8,128)(2,1)S(1)} collective-permute-done((bf16[512,1024]{1,0:T(8,128)(2,1)S(1)}, bf16[512,1024]{1,0:T(8,128)(2,1)S(1)}, u32[]{:S(2)}, u32[]{:S(2)}) %collective-permute-start.25) | collective-permute-done | bytes 1048608 | tf_op jit(solution)/shard_map/ppermute | solution.py:347
  192.9 4.7 %collective-permute-done.26.refs_2_ = bf16[512,1024]{1,0:T(8,128)(2,1)S(1)} collective-permute-done((bf16[512,1024]{1,0:T(8,128)(2,1)S(1)}, bf16[512,1024]{1,0:T(8,128)(2,1)S(1)}, u32[]{:S(2)}, u32[]{:S(2)}) %collective-permute-start.26) | collective-permute-done | bytes 1048608 | tf_op jit(solution)/shard_map/ppermute | solution.py:347
  198.6 3.4 %hidden.1.refs_1_ = bf16[512,512]{1,0:T(8,128)(2,1)} custom-call(bf16[512,1024]{1,0:T(8,128)(2,1)} %copy-done.1, bf16[512,1024]{1,0:T(8,128)(2,1)} %copy-done.18, bf16[512,1024]{1,0:T(8,128)(2,1)} %copy-done.19, bf16[512,128]{1,0:T(8,128)(2,1)} %copy-done.6), custom_call_target="tpu_custom_call" | custom-call | flops 1000000000 | bytes 2097152 | tf_op jit(solution)/shard_map/hidden/pallas_call | solution.py:223
  202.0 1.7 collective-permute-start.31
  203.8 4.8 %down.4 = (bf16[128,1024]{1,0:T(8,128)(2,1)S(1)}, bf16[128,1024]{1,0:T(8,128)(2,1)S(1)}, bf16[128,1024]{1,0:T(8,128)(2,1)S(1)}, bf16[128,1024]{1,0:T(8,128)(2,1)S(1)}) custom-call(s32[3]{0:T(128)S(1)} %copy-done.8, bf16[512,512]{1,0:T(8,128)(2,1)} %hidden.1.refs_1_, bf16[512,128]{1,0:T(8,128)(2,1)S(1)} %copy-done.7, ...), custom_call_target="tpu_custom_call" | custom-call | flops 2147483648 | bytes 4194304 | tf_op jit(solution)/shard_map/down/pallas_call | solution.py:271
  212.8 12.9 %collective-permute-done.31.refs_1_ = bf16[512,512]{1,0:T(8,128)(2,1)S(1)} collective-permute-done((bf16[512,512]{1,0:T(8,128)(2,1)}, bf16[512,512]{1,0:T(8,128)(2,1)S(1)}, u32[]{:S(2)}, u32[]{:S(2)}) %collective-permute-start.31) | collective-permute-done | bytes 524320 | tf_op jit(solution)/shard_map/ppermute | solution.py:347
  225.6 2.2 collective-permute-start.39
  227.9 4.6 %down.5 = (bf16[128,1024]{1,0:T(8,128)(2,1)S(1)}, bf16[128,1024]{1,0:T(8,128)(2,1)S(1)}, bf16[128,1024]{1,0:T(8,128)(2,1)S(1)}, bf16[128,1024]{1,0:T(8,128)(2,1)S(1)}) custom-call(s32[3]{0:T(128)S(1)} %copy-done.8, bf16[512,512]{1,0:T(8,128)(2,1)S(1)} %collective-permute-done.31.refs_1_, bf16[512,128]{1,0:T(8,128)(2,1)S(1)} %copy-done.16, ...), custom_call_target="tpu_custom_call" | custom-call | flops 2147483648 | bytes 4194304 | tf_op jit(solution)/shard_map/down/pallas_call | solution.py:271
  235.4 2.1 combine.4.refs_1_
  237.4 4.2 %collective-permute-done.35.refs_1_ = bf16[512,512]{1,0:T(8,128)(2,1)} collective-permute-done((bf16[512,512]{1,0:T(8,128)(2,1)}, bf16[512,512]{1,0:T(8,128)(2,1)}, u32[]{:S(2)}, u32[]{:S(2)}) %collective-permute-start.35) | collective-permute-done | bytes 524320 | tf_op jit(solution)/shard_map/ppermute | solution.py:347
  242.5 4.8 %down.6 = (bf16[128,1024]{1,0:T(8,128)(2,1)S(1)}, bf16[128,1024]{1,0:T(8,128)(2,1)S(1)}, bf16[128,1024]{1,0:T(8,128)(2,1)S(1)}, bf16[128,1024]{1,0:T(8,128)(2,1)S(1)}) custom-call(s32[3]{0:T(128)S(1)} %copy-done.9, bf16[512,512]{1,0:T(8,128)(2,1)} %collective-permute-done.35.refs_1_, bf16[512,128]{1,0:T(8,128)(2,1)S(1)} %copy-done.14, ...), custom_call_target="tpu_custom_call" | custom-call | flops 2147483648 | bytes 4194304 | tf_op jit(solution)/shard_map/down/pallas_call | solution.py:271
  253.9 3.4 %collective-permute-done.36.refs_3_ = bf16[128,1024]{1,0:T(8,128)(2,1)S(1)} collective-permute-done((bf16[128,1024]{1,0:T(8,128)(2,1)S(1)}, bf16[128,1024]{1,0:T(8,128)(2,1)S(1)}, u32[]{:S(2)}, u32[]{:S(2)}) %collective-permute-start.36) | collective-permute-done | bytes 262176 | tf_op jit(solution)/shard_map/ppermute | solution.py:347
  257.3 1.8 collective-permute-start.34
  259.0 5.5 %down.7 = (bf16[128,1024]{1,0:T(8,128)(2,1)S(1)}, bf16[128,1024]{1,0:T(8,128)(2,1)}, bf16[128,1024]{1,0:T(8,128)(2,1)}, bf16[128,1024]{1,0:T(8,128)(2,1)}) custom-call(s32[3]{0:T(128)S(1)} %copy-done.9, bf16[512,512]{1,0:T(8,128)(2,1)S(1)} %collective-permute-done.39.refs_1_, bf16[512,128]{1,0:T(8,128)(2,1)S(1)} %get-tuple-element.144.refs_2_, ...), custom_call_target="tpu_custom_call" | custom-call | flops 2147483648 | bytes 4194304 | tf_op jit(solution)/shard_map/down/pallas_call | solution.py:271
  269.3 1.8 collective-permute-start.44
  271.0 2.1 combine.5
  274.0 2.1 combine.6
  276.2 2.3 collective-permute-done.43.refs_4_
  280.2 2.1 combine.7
  284.2 2.5 collective-permute-start.41
  286.7 6.9 %collective-permute-done.45.refs_4_ = bf16[128,1024]{1,0:T(8,128)(2,1)S(1)} collective-permute-done((bf16[128,1024]{1,0:T(8,128)(2,1)}, bf16[128,1024]{1,0:T(8,128)(2,1)S(1)}, u32[]{:S(2)}, u32[]{:S(2)}) %collective-permute-start.45) | collective-permute-done | bytes 262176 | tf_op jit(solution)/shard_map/ppermute | solution.py:347
  293.6 2.5 collective-permute-done.40.refs_2_
  296.1 9.0 %collective-permute-done.41.refs_3_ = bf16[128,1024]{1,0:T(8,128)(2,1)S(1)} collective-permute-done((bf16[128,1024]{1,0:T(8,128)(2,1)S(1)}, bf16[128,1024]{1,0:T(8,128)(2,1)S(1)}, u32[]{:S(2)}, u32[]{:S(2)}) %collective-permute-start.41) | collective-permute-done | bytes 262176 | tf_op jit(solution)/shard_map/ppermute | solution.py:347
  305.8 2.4 place.1
  (147 shorter events, 50.1 us)
Async XLA Ops:
  3.7 27.3 %collective-permute-start.11 = (bf16[8,128,512]{2,1,0:T(8,128)(2,1)}, bf16[8,128,512]{2,1,0:T(8,128)(2,1)}, u32[]{:S(2)}, u32[]{:S(2)}) collective-permute-start(bf16[8,128,512]{2,1,0:T(8,128)(2,1)} %pad_maximum_fusion.3), channel_id=1, source_target_pairs={{0,8},{1,9},{2,10},{3,11},{4,12},{5,13},{6,14},{7,15},{8,0},{9,1},... | collective-permute-start | bytes 3145736 | tf_op jit(solution)/shard_map/ppermute | solution.py:347
  7.8 47.4 %collective-permute-start.12 = (bf16[8,128,512]{2,1,0:T(8,128)(2,1)}, bf16[8,128,512]{2,1,0:T(8,128)(2,1)}, u32[]{:S(2)}, u32[]{:S(2)}) collective-permute-start(bf16[8,128,512]{2,1,0:T(8,128)(2,1)} %pad_maximum_fusion.4), channel_id=1, source_target_pairs={{0,16},{1,17},{2,18},{3,19},{4,20},{5,21},{6,22},{7,23},{8,24},{9,... | collective-permute-start | bytes 3145736 | tf_op jit(solution)/shard_map/ppermute | solution.py:347
  10.4 44.8 %collective-permute-start.13 = (bf16[8,128,512]{2,1,0:T(8,128)(2,1)}, bf16[8,128,512]{2,1,0:T(8,128)(2,1)}, u32[]{:S(2)}, u32[]{:S(2)}) collective-permute-start(bf16[8,128,512]{2,1,0:T(8,128)(2,1)} %pad_maximum_fusion.5), channel_id=1, source_target_pairs={{0,24},{1,25},{2,26},{3,27},{4,28},{5,29},{6,30},{7,31},{8,16},{9,... | collective-permute-start | bytes 3145736 | tf_op jit(solution)/shard_map/ppermute | solution.py:347
  57.4 52.0 %copy-start.10 = (bf16[128,1152]{1,0:T(8,128)(2,1)S(1)}, bf16[128,1152]{1,0:T(8,128)(2,1)}, u32[]{:S(2)}) copy-start(bf16[128,1152]{1,0:T(8,128)(2,1)} %get-tuple-element.108.refs_1_) | copy-start | bytes 884740
  57.4 33.0 %collective-permute-start.14 = (bf16[4,8,128,512]{3,2,1,0:T(8,128)(2,1)S(1)}, bf16[4,8,128,512]{3,2,1,0:T(8,128)(2,1)S(1)}, u32[]{:S(2)}, u32[]{:S(2)}) collective-permute-start(bf16[4,8,128,512]{3,2,1,0:T(8,128)(2,1)S(1)} %pad_maximum_fusion.refs_5_), channel_id=1, source_target_pairs={{0,1},{1,0},{2,3},{3,2},{4,5},{5,4},{6,7},{7,6},{8,9},{9,8},{10,11... | collective-permute-start | bytes 12582920 | tf_op jit(solution)/shard_map/ppermute | solution.py:347
  57.5 11.8 %collective-permute-start.7 = (bf16[128,1152]{1,0:T(8,128)(2,1)S(1)}, bf16[128,1152]{1,0:T(8,128)(2,1)S(1)}, u32[]{:S(2)}, u32[]{:S(2)}) collective-permute-start(bf16[128,1152]{1,0:T(8,128)(2,1)S(1)} %copy-done.37), channel_id=1, source_target_pairs={{0,6},{1,7},{2,4},{3,5},{4,2},{5,3},{6,0},{7,1},{8,14},{9,15},{10,... | collective-permute-start | bytes 884744 | tf_op jit(solution)/shard_map/ppermute | solution.py:347
  61.2 25.7 %collective-permute-start.3 = (bf16[128,1152]{1,0:T(8,128)(2,1)S(1)}, bf16[128,1152]{1,0:T(8,128)(2,1)S(1)}, u32[]{:S(2)}, u32[]{:S(2)}) collective-permute-start(bf16[128,1152]{1,0:T(8,128)(2,1)S(1)} %copy-done.36), channel_id=1, source_target_pairs={{0,4},{1,5},{2,6},{3,7},{4,0},{5,1},{6,2},{7,3},{8,12},{9,13},{10,... | collective-permute-start | bytes 884744 | tf_op jit(solution)/shard_map/ppermute | solution.py:347
  69.4 17.5 %collective-permute-start.10 = (bf16[128,1152]{1,0:T(8,128)(2,1)S(1)}, bf16[128,1152]{1,0:T(8,128)(2,1)S(1)}, u32[]{:S(2)}, u32[]{:S(2)}) collective-permute-start(bf16[128,1152]{1,0:T(8,128)(2,1)S(1)} %collective-permute-done.7.refs_1_), channel_id=1, source_target_pairs={{0,24},{1,25},{2,26},{3,27},{4,28},{5,29},{6,30},{7,31},{8,16},{9,... | collective-permute-start | bytes 884744 | tf_op jit(solution)/shard_map/ppermute | solution.py:347
  70.9 16.7 %collective-permute-start.8 = (bf16[128,1152]{1,0:T(8,128)(2,1)S(1)}, bf16[128,1152]{1,0:T(8,128)(2,1)S(1)}, u32[]{:S(2)}, u32[]{:S(2)}) collective-permute-start(bf16[128,1152]{1,0:T(8,128)(2,1)S(1)} %collective-permute-done.7.refs_1_), channel_id=1, source_target_pairs={{0,8},{1,9},{2,10},{3,11},{4,12},{5,13},{6,14},{7,15},{8,0},{9,1},... | collective-permute-start | bytes 884744 | tf_op jit(solution)/shard_map/ppermute | solution.py:347
  72.4 16.7 %collective-permute-start.9 = (bf16[128,1152]{1,0:T(8,128)(2,1)S(1)}, bf16[128,1152]{1,0:T(8,128)(2,1)S(1)}, u32[]{:S(2)}, u32[]{:S(2)}) collective-permute-start(bf16[128,1152]{1,0:T(8,128)(2,1)S(1)} %collective-permute-done.7.refs_1_), channel_id=1, source_target_pairs={{0,16},{1,17},{2,18},{3,19},{4,20},{5,21},{6,22},{7,23},{8,24},{9,... | collective-permute-start | bytes 884744 | tf_op jit(solution)/shard_map/ppermute | solution.py:347
  86.9 22.5 %collective-permute-start.16 = (bf16[128,1152]{1,0:T(8,128)(2,1)S(1)}, bf16[128,1152]{1,0:T(8,128)(2,1)S(1)}, u32[]{:S(2)}, u32[]{:S(2)}) collective-permute-start(bf16[128,1152]{1,0:T(8,128)(2,1)S(1)} %copy-done.35), channel_id=1, source_target_pairs={{0,2},{1,3},{2,0},{3,1},{4,6},{5,7},{6,4},{7,5},{8,10},{9,11},{10,... | collective-permute-start | bytes 884744 | tf_op jit(solution)/shard_map/ppermute | solution.py:347
  86.9 24.0 %collective-permute-start.4 = (bf16[128,1152]{1,0:T(8,128)(2,1)S(1)}, bf16[128,1152]{1,0:T(8,128)(2,1)S(1)}, u32[]{:S(2)}, u32[]{:S(2)}) collective-permute-start(bf16[128,1152]{1,0:T(8,128)(2,1)S(1)} %collective-permute-done.3.refs_1_), channel_id=1, source_target_pairs={{0,8},{1,9},{2,10},{3,11},{4,12},{5,13},{6,14},{7,15},{8,0},{9,1},... | collective-permute-start | bytes 884744 | tf_op jit(solution)/shard_map/ppermute | solution.py:347
  87.5 24.0 %collective-permute-start.5 = (bf16[128,1152]{1,0:T(8,128)(2,1)S(1)}, bf16[128,1152]{1,0:T(8,128)(2,1)S(1)}, u32[]{:S(2)}, u32[]{:S(2)}) collective-permute-start(bf16[128,1152]{1,0:T(8,128)(2,1)S(1)} %collective-permute-done.3.refs_1_), channel_id=1, source_target_pairs={{0,16},{1,17},{2,18},{3,19},{4,20},{5,21},{6,22},{7,23},{8,24},{9,... | collective-permute-start | bytes 884744 | tf_op jit(solution)/shard_map/ppermute | solution.py:347
  89.0 23.0 %collective-permute-start.6 = (bf16[128,1152]{1,0:T(8,128)(2,1)S(1)}, bf16[128,1152]{1,0:T(8,128)(2,1)S(1)}, u32[]{:S(2)}, u32[]{:S(2)}) collective-permute-start(bf16[128,1152]{1,0:T(8,128)(2,1)S(1)} %collective-permute-done.3.refs_1_), channel_id=1, source_target_pairs={{0,24},{1,25},{2,26},{3,27},{4,28},{5,29},{6,30},{7,31},{8,16},{9,... | collective-permute-start | bytes 884744 | tf_op jit(solution)/shard_map/ppermute | solution.py:347
  97.0 40.6 %collective-permute-start.15 = (bf16[512,1024]{1,0:T(8,128)(2,1)S(1)}, bf16[512,1024]{1,0:T(8,128)(2,1)S(1)}, u32[]{:S(2)}, u32[]{:S(2)}) collective-permute-start(bf16[512,1024]{1,0:T(8,128)(2,1)S(1)} %get-tuple-element.96), channel_id=1, source_target_pairs={{0,2},{1,3},{6,4},{7,5},{8,10},{9,11},{14,12},{15,13},{16,18},{17,... | collective-permute-start | bytes 3145736 | tf_op jit(solution)/shard_map/ppermute | solution.py:347
  109.4 34.4 %collective-permute-start = (bf16[128,1152]{1,0:T(8,128)(2,1)S(1)}, bf16[128,1152]{1,0:T(8,128)(2,1)S(1)}, u32[]{:S(2)}, u32[]{:S(2)}) collective-permute-start(bf16[128,1152]{1,0:T(8,128)(2,1)S(1)} %copy-done.10), channel_id=1, source_target_pairs={{0,8},{1,9},{2,10},{3,11},{4,12},{5,13},{6,14},{7,15},{8,0},{9,1},... | collective-permute-start | bytes 884744 | tf_op jit(solution)/shard_map/ppermute | solution.py:347
  111.0 14.7 %collective-permute-start.17 = (bf16[128,1152]{1,0:T(8,128)(2,1)S(1)}, bf16[128,1152]{1,0:T(8,128)(2,1)S(1)}, u32[]{:S(2)}, u32[]{:S(2)}) collective-permute-start(bf16[128,1152]{1,0:T(8,128)(2,1)S(1)} %collective-permute-done.16.refs_1_), channel_id=1, source_target_pairs={{0,8},{1,9},{2,10},{3,11},{4,12},{5,13},{6,14},{7,15},{8,0},{9,1},... | collective-permute-start | bytes 884744 | tf_op jit(solution)/shard_map/ppermute | solution.py:347
  111.5 14.7 %collective-permute-start.18 = (bf16[128,1152]{1,0:T(8,128)(2,1)S(1)}, bf16[128,1152]{1,0:T(8,128)(2,1)S(1)}, u32[]{:S(2)}, u32[]{:S(2)}) collective-permute-start(bf16[128,1152]{1,0:T(8,128)(2,1)S(1)} %collective-permute-done.16.refs_1_), channel_id=1, source_target_pairs={{0,16},{1,17},{2,18},{3,19},{4,20},{5,21},{6,22},{7,23},{8,24},{9,... | collective-permute-start | bytes 884744 | tf_op jit(solution)/shard_map/ppermute | solution.py:347
  112.0 19.1 %collective-permute-start.19 = (bf16[128,1152]{1,0:T(8,128)(2,1)S(1)}, bf16[128,1152]{1,0:T(8,128)(2,1)S(1)}, u32[]{:S(2)}, u32[]{:S(2)}) collective-permute-start(bf16[128,1152]{1,0:T(8,128)(2,1)S(1)} %collective-permute-done.16.refs_1_), channel_id=1, source_target_pairs={{0,24},{1,25},{2,26},{3,27},{4,28},{5,29},{6,30},{7,31},{8,16},{9,... | collective-permute-start | bytes 884744 | tf_op jit(solution)/shard_map/ppermute | solution.py:347
  125.7 19.1 %collective-permute-start.1 = (bf16[128,1152]{1,0:T(8,128)(2,1)S(1)}, bf16[128,1152]{1,0:T(8,128)(2,1)S(1)}, u32[]{:S(2)}, u32[]{:S(2)}) collective-permute-start(bf16[128,1152]{1,0:T(8,128)(2,1)S(1)} %copy-done.10), channel_id=1, source_target_pairs={{0,16},{1,17},{2,18},{3,19},{4,20},{5,21},{6,22},{7,23},{8,24},{9,... | collective-permute-start | bytes 884744 | tf_op jit(solution)/shard_map/ppermute | solution.py:347
  126.2 20.1 %collective-permute-start.2 = (bf16[128,1152]{1,0:T(8,128)(2,1)S(1)}, bf16[128,1152]{1,0:T(8,128)(2,1)S(1)}, u32[]{:S(2)}, u32[]{:S(2)}) collective-permute-start(bf16[128,1152]{1,0:T(8,128)(2,1)S(1)} %copy-done.10), channel_id=1, source_target_pairs={{0,24},{1,25},{2,26},{3,27},{4,28},{5,29},{6,30},{7,31},{8,16},{9,... | collective-permute-start | bytes 884744 | tf_op jit(solution)/shard_map/ppermute | solution.py:347
  139.0 25.5 %collective-permute-start.20 = (bf16[512,1024]{1,0:T(8,128)(2,1)}, bf16[512,1024]{1,0:T(8,128)(2,1)}, u32[]{:S(2)}, u32[]{:S(2)}) collective-permute-start(bf16[512,1024]{1,0:T(8,128)(2,1)} %add_convert_fusion.2), channel_id=1, source_target_pairs={{0,2},{1,3},{2,4},{3,5},{8,10},{9,11},{10,12},{11,13},{16,18},{17,... | collective-permute-start | bytes 3145736 | tf_op jit(solution)/shard_map/ppermute | solution.py:347
  142.1 22.4 %collective-permute-start.21 = (bf16[512,1024]{1,0:T(8,128)(2,1)}, bf16[512,1024]{1,0:T(8,128)(2,1)}, u32[]{:S(2)}, u32[]{:S(2)}) collective-permute-start(bf16[512,1024]{1,0:T(8,128)(2,1)} %add_convert_fusion.2), channel_id=1, source_target_pairs={{4,2},{5,3},{6,4},{7,5},{12,10},{13,11},{14,12},{15,13},{20,18},{2... | collective-permute-start | bytes 3145736 | tf_op jit(solution)/shard_map/ppermute | solution.py:347
  143.8 13.8 %collective-permute-start.22 = (bf16[8,128,256]{2,1,0:T(8,128)(2,1)S(1)}, bf16[8,128,256]{2,1,0:T(8,128)(2,1)S(1)}, u32[]{:S(2)}, u32[]{:S(2)}) collective-permute-start(bf16[8,128,256]{2,1,0:T(8,128)(2,1)S(1)} %get-tuple-element.165), channel_id=1, source_target_pairs={{0,8},{1,9},{2,10},{3,11},{4,12},{5,13},{6,14},{7,15},{8,0},{9,1},... | collective-permute-start | bytes 1572872 | tf_op jit(solution)/shard_map/ppermute | solution.py:347
  144.8 18.0 %collective-permute-start.23 = (bf16[8,128,256]{2,1,0:T(8,128)(2,1)S(1)}, bf16[8,128,256]{2,1,0:T(8,128)(2,1)S(1)}, u32[]{:S(2)}, u32[]{:S(2)}) collective-permute-start(bf16[8,128,256]{2,1,0:T(8,128)(2,1)S(1)} %get-tuple-element.164), channel_id=1, source_target_pairs={{0,16},{1,17},{2,18},{3,19},{4,20},{5,21},{6,22},{7,23},{8,24},{9,... | collective-permute-start | bytes 1572872 | tf_op jit(solution)/shard_map/ppermute | solution.py:347
  146.3 17.8 %collective-permute-start.24 = (bf16[8,128,256]{2,1,0:T(8,128)(2,1)S(1)}, bf16[8,128,256]{2,1,0:T(8,128)(2,1)S(1)}, u32[]{:S(2)}, u32[]{:S(2)}) collective-permute-start(bf16[8,128,256]{2,1,0:T(8,128)(2,1)S(1)} %get-tuple-element.163), channel_id=1, source_target_pairs={{0,24},{1,25},{2,26},{3,27},{4,28},{5,29},{6,30},{7,31},{8,16},{9,... | collective-permute-start | bytes 1572872 | tf_op jit(solution)/shard_map/ppermute | solution.py:347
  164.4 39.4 %collective-permute-start.27 = (bf16[4,8,128,256]{3,2,1,0:T(8,128)(2,1)S(1)}, bf16[4,8,128,256]{3,2,1,0:T(8,128)(2,1)}, u32[]{:S(2)}, u32[]{:S(2)}) collective-permute-start(bf16[4,8,128,256]{3,2,1,0:T(8,128)(2,1)S(1)} %pad_maximum_fusion.1.refs_3_), channel_id=1, source_target_pairs={{0,1},{1,0},{2,3},{3,2},{4,5},{5,4},{6,7},{7,6},{8,9},{9,8},{10,11... | collective-permute-start | bytes 6291464 | tf_op jit(solution)/shard_map/ppermute | solution.py:347
  167.3 36.4 %copy-start.7 = (bf16[512,128]{1,0:T(8,128)(2,1)S(1)}, bf16[512,128]{1,0:T(8,128)(2,1)}, u32[]{:S(2)}) copy-start(bf16[512,128]{1,0:T(8,128)(2,1)} %copy-done.6) | copy-start | bytes 393220
  167.4 25.5 %collective-permute-start.25 = (bf16[512,1024]{1,0:T(8,128)(2,1)S(1)}, bf16[512,1024]{1,0:T(8,128)(2,1)S(1)}, u32[]{:S(2)}, u32[]{:S(2)}) collective-permute-start(bf16[512,1024]{1,0:T(8,128)(2,1)S(1)} %get-tuple-element.162), channel_id=1, source_target_pairs={{0,2},{1,3},{2,4},{3,5},{4,6},{5,7},{8,10},{9,11},{10,12},{11,13},... | collective-permute-start | bytes 3145736 | tf_op jit(solution)/shard_map/ppermute | solution.py:347
  169.9 27.7 %collective-permute-start.26 = (bf16[512,1024]{1,0:T(8,128)(2,1)S(1)}, bf16[512,1024]{1,0:T(8,128)(2,1)S(1)}, u32[]{:S(2)}, u32[]{:S(2)}) collective-permute-start(bf16[512,1024]{1,0:T(8,128)(2,1)S(1)} %get-tuple-element.161), channel_id=1, source_target_pairs={{2,0},{3,1},{4,2},{5,3},{6,4},{7,5},{10,8},{11,9},{12,10},{13,11},... | collective-permute-start | bytes 3145736 | tf_op jit(solution)/shard_map/ppermute | solution.py:347
  202.0 23.6 %collective-permute-start.31 = (bf16[512,512]{1,0:T(8,128)(2,1)}, bf16[512,512]{1,0:T(8,128)(2,1)S(1)}, u32[]{:S(2)}, u32[]{:S(2)}) collective-permute-start(bf16[512,512]{1,0:T(8,128)(2,1)} %hidden.1.refs_1_), channel_id=1, source_target_pairs={{0,2},{1,3},{2,0},{3,1},{4,6},{5,7},{6,4},{7,5},{8,10},{9,11},{10,... | collective-permute-start | bytes 1572872 | tf_op jit(solution)/shard_map/ppermute | solution.py:347
  203.7 37.9 %collective-permute-start.35 = (bf16[512,512]{1,0:T(8,128)(2,1)}, bf16[512,512]{1,0:T(8,128)(2,1)}, u32[]{:S(2)}, u32[]{:S(2)}) collective-permute-start(bf16[512,512]{1,0:T(8,128)(2,1)} %hidden.1.refs_1_), channel_id=1, source_target_pairs={{0,4},{1,5},{2,6},{3,7},{4,0},{5,1},{6,2},{7,3},{8,12},{9,13},{10,... | collective-permute-start | bytes 1572872 | tf_op jit(solution)/shard_map/ppermute | solution.py:347
  209.3 24.6 %collective-permute-start.28 = (bf16[128,1024]{1,0:T(8,128)(2,1)S(1)}, bf16[128,1024]{1,0:T(8,128)(2,1)S(1)}, u32[]{:S(2)}, u32[]{:S(2)}) collective-permute-start(bf16[128,1024]{1,0:T(8,128)(2,1)S(1)} %get-tuple-element.124), channel_id=1, source_target_pairs={{0,8},{1,9},{2,10},{3,11},{4,12},{5,13},{6,14},{7,15},{8,0},{9,1},... | collective-permute-start | bytes 786440 | tf_op jit(solution)/shard_map/ppermute | solution.py:347
  210.1 23.8 %collective-permute-start.29 = (bf16[128,1024]{1,0:T(8,128)(2,1)S(1)}, bf16[128,1024]{1,0:T(8,128)(2,1)S(1)}, u32[]{:S(2)}, u32[]{:S(2)}) collective-permute-start(bf16[128,1024]{1,0:T(8,128)(2,1)S(1)} %get-tuple-element.125), channel_id=1, source_target_pairs={{0,16},{1,17},{2,18},{3,19},{4,20},{5,21},{6,22},{7,23},{8,24},{9,... | collective-permute-start | bytes 786440 | tf_op jit(solution)/shard_map/ppermute | solution.py:347
  211.6 22.3 %collective-permute-start.30 = (bf16[128,1024]{1,0:T(8,128)(2,1)S(1)}, bf16[128,1024]{1,0:T(8,128)(2,1)S(1)}, u32[]{:S(2)}, u32[]{:S(2)}) collective-permute-start(bf16[128,1024]{1,0:T(8,128)(2,1)S(1)} %get-tuple-element.126), channel_id=1, source_target_pairs={{0,24},{1,25},{2,26},{3,27},{4,28},{5,29},{6,30},{7,31},{8,16},{9,... | collective-permute-start | bytes 786440 | tf_op jit(solution)/shard_map/ppermute | solution.py:347
  225.6 26.8 %collective-permute-start.39 = (bf16[512,512]{1,0:T(8,128)(2,1)}, bf16[512,512]{1,0:T(8,128)(2,1)S(1)}, u32[]{:S(2)}, u32[]{:S(2)}) collective-permute-start(bf16[512,512]{1,0:T(8,128)(2,1)} %hidden.1.refs_1_), channel_id=1, source_target_pairs={{0,6},{1,7},{2,4},{3,5},{4,2},{5,3},{6,0},{7,1},{8,14},{9,15},{10,... | collective-permute-start | bytes 1572872 | tf_op jit(solution)/shard_map/ppermute | solution.py:347
  248.1 9.2 %collective-permute-start.36 = (bf16[128,1024]{1,0:T(8,128)(2,1)S(1)}, bf16[128,1024]{1,0:T(8,128)(2,1)S(1)}, u32[]{:S(2)}, u32[]{:S(2)}) collective-permute-start(bf16[128,1024]{1,0:T(8,128)(2,1)S(1)} %get-tuple-element.140), channel_id=1, source_target_pairs={{0,8},{1,9},{2,10},{3,11},{4,12},{5,13},{6,14},{7,15},{8,0},{9,1},... | collective-permute-start | bytes 786440 | tf_op jit(solution)/shard_map/ppermute | solution.py:347
  248.9 16.3 %collective-permute-start.37 = (bf16[128,1024]{1,0:T(8,128)(2,1)S(1)}, bf16[128,1024]{1,0:T(8,128)(2,1)S(1)}, u32[]{:S(2)}, u32[]{:S(2)}) collective-permute-start(bf16[128,1024]{1,0:T(8,128)(2,1)S(1)} %get-tuple-element.141), channel_id=1, source_target_pairs={{0,16},{1,17},{2,18},{3,19},{4,20},{5,21},{6,22},{7,23},{8,24},{9,... | collective-permute-start | bytes 786440 | tf_op jit(solution)/shard_map/ppermute | solution.py:347
  250.4 15.6 %collective-permute-start.38 = (bf16[128,1024]{1,0:T(8,128)(2,1)S(1)}, bf16[128,1024]{1,0:T(8,128)(2,1)S(1)}, u32[]{:S(2)}, u32[]{:S(2)}) collective-permute-start(bf16[128,1024]{1,0:T(8,128)(2,1)S(1)} %get-tuple-element.142), channel_id=1, source_target_pairs={{0,24},{1,25},{2,26},{3,27},{4,28},{5,29},{6,30},{7,31},{8,16},{9,... | collective-permute-start | bytes 786440 | tf_op jit(solution)/shard_map/ppermute | solution.py:347
  251.6 17.0 %collective-permute-start.32 = (bf16[128,1024]{1,0:T(8,128)(2,1)S(1)}, bf16[128,1024]{1,0:T(8,128)(2,1)S(1)}, u32[]{:S(2)}, u32[]{:S(2)}) collective-permute-start(bf16[128,1024]{1,0:T(8,128)(2,1)S(1)} %copy-done.12), channel_id=1, source_target_pairs={{0,8},{1,9},{2,10},{3,11},{4,12},{5,13},{6,14},{7,15},{8,0},{9,1},... | collective-permute-start | bytes 786440 | tf_op jit(solution)/shard_map/ppermute | solution.py:347
  252.4 20.7 %collective-permute-start.33 = (bf16[128,1024]{1,0:T(8,128)(2,1)S(1)}, bf16[128,1024]{1,0:T(8,128)(2,1)}, u32[]{:S(2)}, u32[]{:S(2)}) collective-permute-start(bf16[128,1024]{1,0:T(8,128)(2,1)S(1)} %get-tuple-element.131), channel_id=1, source_target_pairs={{0,16},{1,17},{2,18},{3,19},{4,20},{5,21},{6,22},{7,23},{8,24},{9,... | collective-permute-start | bytes 786440 | tf_op jit(solution)/shard_map/ppermute | solution.py:347
  257.3 16.8 %collective-permute-start.34 = (bf16[128,1024]{1,0:T(8,128)(2,1)S(1)}, bf16[128,1024]{1,0:T(8,128)(2,1)}, u32[]{:S(2)}, u32[]{:S(2)}) collective-permute-start(bf16[128,1024]{1,0:T(8,128)(2,1)S(1)} %get-tuple-element.132), channel_id=1, source_target_pairs={{0,24},{1,25},{2,26},{3,27},{4,28},{5,29},{6,30},{7,31},{8,16},{9,... | collective-permute-start | bytes 786440 | tf_op jit(solution)/shard_map/ppermute | solution.py:347
  265.2 10.9 %collective-permute-start.42 = (bf16[128,1024]{1,0:T(8,128)(2,1)}, bf16[128,1024]{1,0:T(8,128)(2,1)S(1)}, u32[]{:S(2)}, u32[]{:S(2)}) collective-permute-start(bf16[128,1024]{1,0:T(8,128)(2,1)} %get-tuple-element.146), channel_id=1, source_target_pairs={{0,8},{1,9},{2,10},{3,11},{4,12},{5,13},{6,14},{7,15},{8,0},{9,1},... | collective-permute-start | bytes 786440 | tf_op jit(solution)/shard_map/ppermute | solution.py:347
  266.0 12.5 %collective-permute-start.43 = (bf16[128,1024]{1,0:T(8,128)(2,1)}, bf16[128,1024]{1,0:T(8,128)(2,1)S(1)}, u32[]{:S(2)}, u32[]{:S(2)}) collective-permute-start(bf16[128,1024]{1,0:T(8,128)(2,1)} %get-tuple-element.147), channel_id=1, source_target_pairs={{0,16},{1,17},{2,18},{3,19},{4,20},{5,21},{6,22},{7,23},{8,24},{9,... | collective-permute-start | bytes 786440 | tf_op jit(solution)/shard_map/ppermute | solution.py:347
  269.3 10.2 %collective-permute-start.44 = (bf16[128,1024]{1,0:T(8,128)(2,1)}, bf16[128,1024]{1,0:T(8,128)(2,1)S(1)}, u32[]{:S(2)}, u32[]{:S(2)}) collective-permute-start(bf16[128,1024]{1,0:T(8,128)(2,1)} %get-tuple-element.148), channel_id=1, source_target_pairs={{0,24},{1,25},{2,26},{3,27},{4,28},{5,29},{6,30},{7,31},{8,16},{9,... | collective-permute-start | bytes 786440 | tf_op jit(solution)/shard_map/ppermute | solution.py:347
  282.3 11.3 %collective-permute-start.45 = (bf16[128,1024]{1,0:T(8,128)(2,1)}, bf16[128,1024]{1,0:T(8,128)(2,1)S(1)}, u32[]{:S(2)}, u32[]{:S(2)}) collective-permute-start(bf16[128,1024]{1,0:T(8,128)(2,1)} %combine.7), channel_id=1, source_target_pairs={{0,6},{1,7},{2,4},{3,5},{4,2},{5,3},{6,0},{7,1},{8,14},{9,15},{10,... | collective-permute-start | bytes 786440 | tf_op jit(solution)/shard_map/ppermute | solution.py:347
  283.8 12.2 %collective-permute-start.40 = (bf16[128,1024]{1,0:T(8,128)(2,1)}, bf16[128,1024]{1,0:T(8,128)(2,1)S(1)}, u32[]{:S(2)}, u32[]{:S(2)}) collective-permute-start(bf16[128,1024]{1,0:T(8,128)(2,1)} %combine.6), channel_id=1, source_target_pairs={{0,2},{1,3},{2,0},{3,1},{4,6},{5,7},{6,4},{7,5},{8,10},{9,11},{10,... | collective-permute-start | bytes 786440 | tf_op jit(solution)/shard_map/ppermute | solution.py:347
  284.2 20.9 %collective-permute-start.41 = (bf16[128,1024]{1,0:T(8,128)(2,1)S(1)}, bf16[128,1024]{1,0:T(8,128)(2,1)S(1)}, u32[]{:S(2)}, u32[]{:S(2)}) collective-permute-start(bf16[128,1024]{1,0:T(8,128)(2,1)S(1)} %copy-done.24), channel_id=1, source_target_pairs={{0,4},{1,5},{2,6},{3,7},{4,0},{5,1},{6,2},{7,3},{8,12},{9,13},{10,... | collective-permute-start | bytes 786440 | tf_op jit(solution)/shard_map/ppermute | solution.py:347
  (36 other events, 254.6 us)
